TPU v7x, 256 devices: a whole 4x4x8 slice. The times are simulated.
256 devices in a mesh: dp: 64 (over z, y, core), tp: 4 (over x).
Axes of the slice: x: 4, y: 4, z: 8, core: 2. Of those that a mesh axis runs over, the one named last changes fastest.
Arguments:
- partial_up: bfloat16 [64, 1024, 4096], P('dp', None, 'tp'), may hold values from -8 to 8
- partial_down: bfloat16 [64, 4096, 1024], P('dp', 'tp'), may hold values from -8 to 8
- partial_norm: bfloat16 [64, 1024], P('dp'), may hold values from -16 to 16
- master_up: float32 [1024, 4096], P('dp', 'tp'), may hold values from -0.5 to 0.5
- master_down: float32 [4096, 1024], P('tp', 'dp'), may hold values from -0.25 to 0.25
- master_norm: float32 [1024], P('dp'), may hold values from 0.25 to 1.75
- memory_up: float32 [1024, 4096], P('dp', 'tp'), may hold values from 0.0001953125 to 0.001953125
- memory_down: float32 [4096, 1024], P('tp', 'dp'), may hold values from 4.8828126e-05 to 0.00048828125
- memory_norm: float32 [1024], P('dp'), may hold values from 0.05 to 0.8
Outputs:
- compute_up: bfloat16 [1024, 4096], P(None, 'tp')
- compute_down: bfloat16 [4096, 1024], P('tp')
- compute_norm: bfloat16 [1024], replicated
- stepped_up: float32 [1024, 4096], P('dp', 'tp')
- stepped_down: float32 [4096, 1024], P('tp', 'dp')
- stepped_norm: float32 [1024], P('dp')
- state_new_up: float32 [1024, 4096], P('dp', 'tp')
- state_new_down: float32 [4096, 1024], P('tp', 'dp')
- state_new_norm: float32 [1024], P('dp')
All inputs are finite; a program needn't handle non-finite values.
Results may differ from a plain program's by a relative error of at most 0.001.
Values may be sent and summed in bfloat16 or wider, within the bound.
A program may use at most 64 MiB of HBM per device.

v0:
```python
import jax
import jax.numpy as jnp
from jax import lax
from jax.sharding import Mesh
from jax.sharding import PartitionSpec as P

DP = ("dp_0", "dp_1", "dp_2")


learn_rate = 0.025
hold_rate = 0.8


def cut_along(array, dim, size):
    before, after = (array.shape[:dim], array.shape[dim + 1 :])
    return jnp.moveaxis(array.reshape(*before, size, -1, *after), dim, 0)


def sum_packed(arrays, axis, dims):
    size = lax.axis_size(axis)
    pieces = [cut_along(a, dim, size) for a, dim in zip(arrays, dims)]
    lines = jnp.concatenate([b.reshape(size, -1) for b in pieces], axis=1)
    width = max(16, -(-lines.shape[1] // 1024) * 8)
    lines = jnp.pad(lines, ((0, 0), (0, width * 128 - lines.shape[1]))).reshape(-1, 128)
    vector, at, gathered = (lax.psum_scatter(lines, axis, tiled=True).reshape(-1), 0, [])
    for b in pieces:
        part = b[0]
        gathered.append(vector[at : at + part.size].reshape(part.shape))
        at += part.size
    return tuple(gathered)


def over_axes(array, axes):
    for axis in axes:
        array = lax.psum(array, axis)
    return array


def sent_to_all(array, axis):
    copies = jnp.broadcast_to(array, (lax.axis_size(axis), *array.shape))
    return lax.all_to_all(copies, axis, split_axis=0, concat_axis=0, tiled=True)


def of_everyone(array, axis):
    everything = sent_to_all(array, axis)
    return jnp.sum(everything, axis=0)


def in_one(arrays, axis):
    ends = [0]
    for a in arrays:
        ends.append(ends[-1] + a.size)
    running = of_everyone(jnp.concatenate([a.ravel() for a in arrays]), axis)
    return tuple((running[b:e].reshape(a.shape) for a, b, e in zip(arrays, ends, ends[1:])))


def turned_gather(arrays, axis, dims):
    turned = [jnp.moveaxis(a, dim, 0) for a, dim in zip(arrays, dims)]
    widths = [t[0].size for t in turned]
    both = jnp.concatenate([t.reshape(-1, w) for t, w in zip(turned, widths)], axis=1)
    filled = lax.all_gather(both, axis, axis=0, tiled=True)
    pieces = jnp.split(filled, [sum(widths[:k]) for k in range(1, len(widths))], axis=1)
    return tuple(
        (
            jnp.moveaxis(b.reshape(-1, *t.shape[1:]), 0, dim)
            for b, t, dim in zip(pieces, turned, dims)
        )
    )


def local(
    partial_up,
    partial_down,
    partial_norm,
    master_up,
    master_down,
    master_norm,
    memory_up,
    memory_down,
    memory_norm,
):
    mean_up, mean_down = sum_packed(
        (partial_up[0].astype(jnp.float32), partial_down[0].astype(jnp.float32)), DP, (0, 1)
    )
    whole_norm = over_axes(partial_norm[0].astype(jnp.float32), DP)
    place = lax.axis_index(DP)
    mean_norm = lax.dynamic_slice_in_dim(
        whole_norm, place * master_norm.shape[0], master_norm.shape[0]
    )
    mean_rate = lax.axis_size(DP) ** (-0.5)
    mean_up = mean_up * mean_rate
    mean_down = mean_down * mean_rate
    mean_norm = mean_norm * mean_rate
    own_up, own_down, slope_up_norm, slope_down_norm = in_one(
        (
            jnp.sum(master_up * master_up, axis=1, keepdims=True),
            jnp.sum(master_down * master_down, axis=0, keepdims=True),
            jnp.sum(mean_up * mean_up, axis=1, keepdims=True),
            jnp.sum(mean_down * mean_down, axis=0, keepdims=True),
        ),
        "tp",
    )
    mean_up = mean_up * (jnp.sqrt(own_up) * lax.rsqrt(slope_up_norm + 1e-06))
    mean_down = mean_down * (jnp.sqrt(own_down) * lax.rsqrt(slope_down_norm + 1e-06))
    state_new_up = hold_rate * memory_up + (1.0 - hold_rate) * mean_up * mean_up
    stepped_up = master_up - learn_rate * mean_up * lax.rsqrt(state_new_up + 1e-06)
    state_new_down = hold_rate * memory_down + (1.0 - hold_rate) * mean_down * mean_down
    stepped_down = master_down - learn_rate * mean_down * lax.rsqrt(state_new_down + 1e-06)
    state_new_norm = hold_rate * memory_norm + (1.0 - hold_rate) * mean_norm * mean_norm
    stepped_norm = master_norm - learn_rate * mean_norm * lax.rsqrt(state_new_norm + 1e-06)
    compute_up, compute_down, compute_norm = turned_gather(
        (
            stepped_up.astype(jnp.bfloat16),
            stepped_down.astype(jnp.bfloat16),
            stepped_norm.astype(jnp.bfloat16),
        ),
        DP,
        (0, 1, 0),
    )
    return (
        compute_up,
        compute_down,
        compute_norm,
        stepped_up,
        stepped_down,
        stepped_norm,
        state_new_up,
        state_new_down,
        state_new_norm,
    )


def solution(mesh):
    finer = Mesh(mesh.devices.reshape(8, 4, 2, mesh.shape["tp"]), ("dp_0", "dp_1", "dp_2", "tp"))
    return jax.shard_map(
        local,
        mesh=finer,
        in_specs=(
            P(DP, None, "tp"),
            P(DP, "tp", None),
            P(DP, None),
            P(DP, "tp"),
            P("tp", DP),
            P(DP),
            P(DP, "tp"),
            P("tp", DP),
            P(DP),
        ),
        out_specs=(
            P(None, "tp"),
            P("tp", None),
            P(),
            P(DP, "tp"),
            P("tp", DP),
            P(DP),
            P(DP, "tp"),
            P("tp", DP),
            P(DP),
        ),
        check_vma=False,
    )
```

profile of v0, /device:TPU:1, one launch (start us, length us, event | category | flops | bytes accessed | tf_op | source)
XLA Modules:
  0.0 300.1 jit_solution(11367496237568048185)
XLA Ops:
  7.2 2.9 copy.45
  10.1 6.1 %copy.46 = bf16[64,1024,16]{0,2,1:T(8,128)(2,1)} copy(bf16[64,1024,16]{1,2,0:T(8,128)(2,1)S(1)} %bitcast.13) | data formatting | bytes 4194304 | tf_op jit(solution)/shard_map/transpose | solution.py:16
  16.2 3.5 %copy.47 = bf16[64,16384]{1,0:T(8,128)(2,1)S(1)} copy(bf16[64,16384]{0,1:T(8,128)(2,1)} %bitcast.12) | data formatting | bytes 4194304 | tf_op jit(solution)/shard_map/reshape | solution.py:22
  19.8 4.2 %convert_element_type.25 = bf16[64,16384]{1,0:T(8,128)(2,1)} reshape(bf16[1,1024,1024]{2,1,0:T(8,128)(2,1)} %param.9) | data formatting | bytes 4194304 | tf_op jit(solution)/shard_map/convert_element_type | solution.py:83
  23.9 5.3 %maximum_convert_fusion = f32[64,32768]{1,0:T(8,128)} fusion(bf16[64,16384]{1,0:T(8,128)(2,1)S(1)} %copy.47, bf16[64,16384]{1,0:T(8,128)(2,1)} %convert_element_type.25), kind=kLoop, calls=%fused_computation | loop fusion | flops 8388608 | bytes 12582912 | tf_op jit(solution)/shard_map/reshape | solution.py:24
  29.3 9.3 %reshape.81 = f32[16384,128]{1,0:T(8,128)} reshape(f32[64,32768]{1,0:T(8,128)} %maximum_convert_fusion) | data formatting | bytes 16777216 | tf_op jit(solution)/shard_map/reshape | solution.py:24
  38.7 0.6 copy-done.4
  39.3 17.3 %psum.21 = f32[1024]{0:T(1024)S(1)} all-reduce(f32[1024]{0:T(1024)S(1)} %bitcast.14), channel_id=1, replica_groups=mesh['dp_0'=8,'dp_1'=4,'dp_2'=2,'tp'=4] {'dp_0'}, use_global_device_ids=true, to_apply=%region_7.8 | all-reduce | flops 1024 | bytes 8192 | tf_op jit(solution)/shard_map/psum | solution.py:35
  56.6 8.7 %psum.22 = f32[1024]{0:T(1024)S(1)} all-reduce(f32[1024]{0:T(1024)S(1)} %psum.21), channel_id=1, replica_groups=mesh['dp_0'=8,'dp_1'=4,'dp_2'=2,'tp'=4] {'dp_1'}, use_global_device_ids=true, to_apply=%region_8.9 | all-reduce | flops 1024 | bytes 8192 | tf_op jit(solution)/shard_map/psum | solution.py:35
  65.3 8.3 %psum.23 = f32[1024]{0:T(1024)S(1)} all-reduce(f32[1024]{0:T(1024)S(1)} %psum.22), channel_id=1, replica_groups=mesh['dp_0'=8,'dp_1'=4,'dp_2'=2,'tp'=4] {'dp_2'}, use_global_device_ids=true, to_apply=%region_9.10 | all-reduce | flops 1024 | bytes 8192 | tf_op jit(solution)/shard_map/psum | solution.py:35
  73.6 0.1 multiply_reduce_fusion.2
  73.8 0.1 multiply_reduce_fusion.3
  73.9 116.3 %reduce-scatter.2.cloned.1.call-done = f32[256,128]{1,0:T(8,128)} async-done(((f32[16384,128]{1,0:T(8,128)}), f32[256,128]{1,0:T(8,128)}) %reduce-scatter.2.cloned.1.call-update) | async-done | bytes 131088 | tf_op jit(solution)/shard_map/reduce_scatter | solution.py:25
  190.1 1.0 fusion.5
  191.1 0.2 reshape.77
  191.3 0.2 multiply_reduce_fusion
  191.5 0.1 reduce_sum.55
  191.5 0.1 reduce_sum.56
  191.7 0.6 broadcast_in_dim.3
  192.3 4.4 %all-to-all-start = ((f32[4,1,64]{2,1,0:T(1,128)}), f32[4,1,64]{2,1,0:T(1,128)S(1)}, u32[]{:S(2)}, u32[]{:S(2)}) async-start(f32[4,1,64]{2,1,0:T(1,128)} %broadcast_in_dim.3), calls=%async_computation.1 | async-start | bytes 4096 | tf_op jit(solution)/shard_map/all_to_all | solution.py:41
  196.7 0.6 convert_bitcast_fusion.1
  197.3 0.1 copy.50
  197.4 0.2 copy.49
  197.6 3.2 %all-to-all-done = f32[4,1,64]{2,1,0:T(1,128)S(1)} async-done(((f32[4,1,64]{2,1,0:T(1,128)}), f32[4,1,64]{2,1,0:T(1,128)S(1)}, u32[]{:S(2)}, u32[]{:S(2)}) %all-to-all-start) | async-done | bytes 1056 | tf_op jit(solution)/shard_map/all_to_all | solution.py:41
  200.8 0.1 multiply_multiply_fusion.3
  200.9 0.7 convert_bitcast_fusion
  201.6 0.7 fusion.2
  202.4 0.6 pad_maximum_fusion
  203.0 82.0 %all-gather.2.cloned.1.call-done = bf16[1024,2049]{1,0:T(8,128)(2,1)} async-done(((bf16[16,2049]{1,0:T(8,128)(2,1)}), bf16[1024,2049]{1,0:T(8,128)(2,1)}) %all-gather.2.cloned.1.call-update) | async-done | bytes 4196368 | tf_op jit(solution)/shard_map/all_gather | solution.py:61
  285.0 4.0 %slice_bitcast_fusion = (bf16[1024,1024]{0,1:T(8,128)(2,1)S(1)}, bf16[1024,1024]{1,0:T(8,128)(2,1)}) fusion(bf16[1024,2049]{1,0:T(8,128)(2,1)} %all-gather.2.cloned.1.call-done), kind=kLoop, calls=%fused_computation.1 | loop fusion | bytes 8388608 | tf_op jit(solution)/shard_map/transpose | solution.py:65
  289.0 2.5 copy.51
  291.6 1.7 slice_reduce_fusion
  (21 shorter events, 0.2 us)
Async XLA Ops:
  7.2 183.0 %reduce-scatter.2.cloned.1.call-start = ((), (), s32[]{:S(2)}) async-start(), calls=%async_computation.2 | async-start | bytes 8519680 | tf_op jit(solution)/shard_map/reduce_scatter | solution.py:25
  38.6 0.7 copy-start.4
  38.6 35.0 %copy-start = (f32[1024,16]{0,1:T(8,128)S(1)}, f32[1024,16]{0,1:T(8,128)}, u32[]{:S(2)}) copy-start(f32[1024,16]{0,1:T(8,128)} %param.13) | copy-start | bytes 196612
  38.6 35.2 %copy-start.1 = (f32[16,1024]{1,0:T(8,128)S(1)}, f32[16,1024]{1,0:T(8,128)}, u32[]{:S(2)}) copy-start(f32[16,1024]{1,0:T(8,128)} %param.12) | copy-start | bytes 196612
  38.6 158.1 %copy-start.5 = (f32[16]{0:T(128)S(1)}, f32[16]{0:T(128)}, u32[]{:S(2)}) copy-start(f32[16]{0:T(128)} %param.14) | copy-start | bytes 196
  38.6 158.1 %copy-start.6 = (f32[16]{0:T(128)S(1)}, f32[16]{0:T(128)}, u32[]{:S(2)}) copy-start(f32[16]{0:T(128)} %param.17) | copy-start | bytes 196
  38.6 162.3 %copy-start.2 = (f32[1024,16]{0,1:T(8,128)S(1)}, f32[1024,16]{0,1:T(8,128)}, u32[]{:S(2)}) copy-start(f32[1024,16]{0,1:T(8,128)} %param.16) | copy-start | bytes 196612
  38.6 163.0 %copy-start.3 = (f32[16,1024]{1,0:T(8,128)S(1)}, f32[16,1024]{1,0:T(8,128)}, u32[]{:S(2)}) copy-start(f32[16,1024]{1,0:T(8,128)} %param.15) | copy-start | bytes 196612
  192.3 8.4 %all-to-all-start = ((f32[4,1,64]{2,1,0:T(1,128)}), f32[4,1,64]{2,1,0:T(1,128)S(1)}, u32[]{:S(2)}, u32[]{:S(2)}) async-start(f32[4,1,64]{2,1,0:T(1,128)} %broadcast_in_dim.3), calls=%async_computation.1 | async-start | bytes 4096 | tf_op jit(solution)/shard_map/all_to_all | solution.py:41
  196.7 88.3 %all-gather.2.cloned.1.call-start = ((), (), s32[]{:S(2)}) async-start(), calls=%async_computation.3 | async-start | bytes 4526080 | tf_op jit(solution)/shard_map/all_gather | solution.py:61
Sparse Core Ops, SparseCore 0:
  38.8 151.3 reduce-scatter.1
  203.1 81.8 all-gather.1
where the time goes:
time: 301 us; the launch traced here: 300 us
  waiting for transfers between devices  201 us (67%)
  local copies, waits for them, and re-layouts  36 us (12%)
  blocking collectives  34.4 us (11%)
  between operations  14.1 us (5%)
  other arithmetic  9.73 us (3%)
  starting transfers between devices  4.42 us (1%)
    reduce_scatter x1, waiting for transfers between devices, sum_packed(): lax.psum_scatter(lines, axis, tiled=True).reshape(-1)  116 us
    all_gather x1, waiting for transfers between devices, turned_gather(): filled = lax.all_gather(both, axis, axis=0, tiled=True)  82 us
    psum x3, blocking collectives, over_axes(): array = lax.psum(array, axis)  34.4 us
    reshape x1, local copies, waits for them, and re-layouts, sum_packed(): jnp.pad(lines, ((0, 0), (0, width * 128 - lines.shape[1]))).reshape(-1, 128)  9.28 us
    transpose x1, local copies, waits for them, and re-layouts, cut_along(): return jnp.moveaxis(array.reshape(*before, size, -1, *after), dim, 0)  6.13 us
    unnamed x16, local copies, waits for them, and re-layouts  6.03 us
  transfers between devices with their start and end apart: 3, of which 3 were waited for; matrix products, arithmetic and copies ran while one was open for 0% of the time, Pallas kernels for 0%

commit v1 on v0

v1 whole, which is shorter than its diff:
```python
import functools

import jax
import jax.numpy as jnp
from jax import lax
from jax.experimental import pallas as pl
from jax.experimental.pallas import tpu as pltpu
from jax.sharding import Mesh
from jax.sharding import PartitionSpec as P

DP = ("dp_0", "dp_1", "dp_2")
NZ, NY, NC, NX = 8, 4, 2, 4
MESH = pl.DeviceIdType.MESH
F32, BF16 = jnp.float32, jnp.bfloat16

learn_rate = 0.025
hold_rate = 0.8


def updated(master, memory, mean):
    state = hold_rate * memory + (1.0 - hold_rate) * mean * mean
    return master - learn_rate * mean * lax.rsqrt(state + 1e-06), state


def slots_of(n):
    out = [(n // 2, 0)]
    for k in range(n // 2 - 1, 0, -1):
        out += [(k, 1), (k, 0)]
    return out


def kernel(
    small, pu, pd, mu, md, vu, vd,
    out_u, out_d, nout, su, sd, qu, qd,
    own_u, pr_u, own_d, pr_d, ds, dr, us, ur, sum_u, zs, zr, gs, gr, tps, tpr, gds, gd, sms, smr,
    loc_u, loc_d, s0_send, s0u_recv, s0d_recv, d_send, d_recv, u_send, u_recv, z_send, z_recv,
    g_send, g_recv, t_send, t_recv, sm_send, sm_recv,
    agz_send, agz_recv, agy_send, agy_recv, agd_send, agd_recv, gd_send, gd_recv, pair_send, pair_recv,
):
    z, y, c, x = (lax.axis_index(a) for a in ("dp_0", "dp_1", "dp_2", "tp"))
    o = 1 - c
    zo = lambda k: lax.rem(z + k + NZ, NZ)
    yo = lambda k: lax.rem(y + k + NY, NY)

    def rcopy(src, dst, ssem, rsem, **dev):
        cp = pltpu.make_async_remote_copy(
            src_ref=src, dst_ref=dst, send_sem=ssem, recv_sem=rsem, device_id=dev, device_id_type=MESH
        )
        return cp

    def started(*args, **dev):
        rcopy(*args, **dev).start()

    def arrived(dst, rsem):
        pltpu.make_async_copy(dst, dst, rsem).wait()

    zorder = (4, 3, -3, 2, -2, 1, -1, 0)
    yorder = (2, 1, -1, 0)
    col = lambda zt: pl.ds(pl.multiple_of(zt * 128, 128), 128)
    for i, k in enumerate(zorder):
        pltpu.make_async_copy(pd.at[c, :, col(zo(k))], own_d.at[zo(k)], loc_d.at[i]).start()
    for i, k in enumerate(yorder):
        pltpu.make_async_copy(pu.at[:, yo(k), c], own_u.at[:, yo(k)], loc_u.at[i]).start()

    barrier = pltpu.get_barrier_semaphore()
    peers = [{"dp_0": zo(k)} for k in range(1, NZ)]
    peers += [{"dp_1": yo(dy), "dp_2": lax.rem(c + dc, NC)} for dy in range(NY) for dc in range(NC) if dy or dc]
    peers += [{"tp": lax.rem(x + k, NX)} for k in range(1, NX)]
    for dev in peers:
        pl.semaphore_signal(barrier, inc=1, device_id=dev, device_id_type=MESH)
    pl.semaphore_wait(barrier, len(peers))

    for i in range(8):
        zt = zo(zorder[i])
        started(pd.at[o, :, col(zt)], pr_d.at[zt], s0_send.at[0], s0d_recv.at[i], dp_2=o)
        if i % 2 == 0:
            yt = yo(yorder[i // 2])
            started(pu.at[:, yt, o], pr_u.at[:, yt], s0_send.at[1], s0u_recv.at[i // 2], dp_2=o)
    started(small, smr.at[0], sm_send.at[0], sm_recv.at[0], dp_2=o)

    have = set()

    def need_d(k):
        if ("d", k) not in have:
            have.add(("d", k))
            i = zorder.index(k)
            pltpu.make_async_copy(pd.at[c, :, col(zo(k))], own_d.at[zo(k)], loc_d.at[i]).wait()
            arrived(pr_d.at[zo(k)], s0d_recv.at[i])

    def need_u(k):
        if ("u", k) not in have:
            have.add(("u", k))
            i = yorder.index(k)
            pltpu.make_async_copy(pu.at[:, yo(k), c], own_u.at[:, yo(k)], loc_u.at[i]).wait()
            arrived(pr_u.at[:, yo(k)], s0u_recv.at[i])

    zslots, yslots = slots_of(NZ), slots_of(NY)

    def half_of(direction, h):
        return h if direction == 0 else 1 - h

    def sign(direction):
        return 1 if direction == 0 else -1

    def d_slot(direction, i):
        k, h = zslots[i]
        k = k * sign(direction)
        kk = 4 if k == -4 else k
        need_d(kk)
        rows = pl.ds(half_of(direction, h) * 256, 256)
        val = own_d[zo(kk), rows].astype(F32) + pr_d[zo(kk), rows].astype(F32)
        if i >= 2:
            arrived(dr.at[direction, i - 2], d_recv.at[direction, i - 2])
            val = val + dr[direction, i - 2]
        ds[direction, i] = val
        started(
            ds.at[direction, i], dr.at[direction, i], d_send.at[direction], d_recv.at[direction, i],
            dp_0=zo(sign(direction)),
        )

    def u_slot(direction, i):
        k, h = yslots[i]
        k = k * sign(direction)
        kk = 2 if k == -2 else k
        need_u(kk)
        part = pl.ds(half_of(direction, h) * 4, 4)
        val = own_u[part, yo(kk)].astype(F32) + pr_u[part, yo(kk)].astype(F32)
        if i >= 2:
            arrived(ur.at[direction, i - 2], u_recv.at[direction, i - 2])
            val = val + ur[direction, i - 2]
        us[direction, i] = val
        started(
            us.at[direction, i], ur.at[direction, i], u_send.at[direction], u_recv.at[direction, i],
            dp_1=yo(sign(direction)),
        )

    def z_slot(direction, i):
        k, h = zslots[i]
        k = k * sign(direction)
        rows = pl.ds(half_of(direction, h) * 8, 8)
        val = sum_u[zo(k), rows]
        if i >= 2:
            arrived(zr.at[direction, i - 2], z_recv.at[direction, i - 2])
            val = val + zr[direction, i - 2]
        zs[direction, i] = val
        started(
            zs.at[direction, i], zr.at[direction, i], z_send.at[direction], z_recv.at[direction, i],
            dp_0=zo(sign(direction)),
        )

    for i in (0, 1):
        for direction in (0, 1):
            d_slot(direction, i)
        for direction in (0, 1):
            u_slot(direction, i)

    arrived(smr.at[0], sm_recv.at[0])
    sms[0] = small[...] + smr[0]
    for dy in range(1, NY):
        started(sms.at[0], smr.at[dy], sm_send.at[1], sm_recv.at[dy], dp_1=yo(dy))

    for direction in (0, 1):
        d_slot(direction, 2)
    for direction in (0, 1):
        d_slot(direction, 3)
    for direction in (0, 1):
        u_slot(direction, 2)

    total = sms[0]
    for dy in range(1, NY):
        arrived(smr.at[dy], sm_recv.at[dy])
        total = total + smr[dy]
    sms[1] = total
    for k in range(1, NZ):
        started(sms.at[1], smr.at[3 + k], sm_send.at[2], sm_recv.at[3 + k], dp_0=zo(k))

    for i in (4, 5, 6):
        for direction in (0, 1):
            d_slot(direction, i)

    total = sms[1]
    for k in range(1, NZ):
        arrived(smr.at[3 + k], sm_recv.at[3 + k])
        total = total + smr[3 + k]
    stepped, state = updated(total[8:16], total[16:24], total[0:8] * 0.125)
    nout[0:8] = stepped
    nout[8:16] = state

    need_u(0)
    for h in (0, 1):
        part = pl.ds(4 * h, 4)
        val = own_u[part, y].astype(F32) + pr_u[part, y].astype(F32)
        for direction in (0, 1):
            i = 2 if half_of(direction, 0) == h else 1
            arrived(ur.at[direction, i], u_recv.at[direction, i])
            val = val + ur[direction, i]
        sum_u[part] = val
    for i in (0, 1):
        for direction in (0, 1):
            z_slot(direction, i)

    need_d(0)
    for h in (0, 1):
        rows = pl.ds(256 * h, 256)
        val = own_d[z, rows].astype(F32) + pr_d[z, rows].astype(F32)
        for direction in (0, 1):
            i = 6 if half_of(direction, 0) == h else 5
            arrived(dr.at[direction, i], d_recv.at[direction, i])
            val = val + dr[direction, i]
        for b in (0, 1):
            gs[:, :, pl.ds(256 * h + 128 * b, 128)] = val[128 * b : 128 * b + 128].T.reshape(NY * NC, 16, 128)
    for dy in range(NY):
        for dc in range(NC):
            if dy or dc:
                yt, ct = yo(dy), lax.rem(c + dc, NC)
                started(
                    gs.at[yt * NC + ct], gr.at[c, dy], g_send.at[0], g_recv.at[dy, dc], dp_1=yt, dp_2=ct
                )
    gr[c, 0] = gs[y * NC + c]

    for i in (2, 3, 4, 5, 6):
        for direction in (0, 1):
            z_slot(direction, i)

    lane = lax.broadcasted_iota(jnp.int32, (16, 128), 1)

    def tp_send(which, mean, master):
        own = jnp.sum(master * master, axis=1, keepdims=True)
        slope = jnp.sum(mean * mean, axis=1, keepdims=True)
        tps[which] = jnp.where(lane < 64, own, slope)
        for k in range(1, NX):
            started(
                tps.at[which], tpr.at[which, k - 1], t_send.at[which], t_recv.at[which, k - 1],
                tp=lax.rem(x + k, NX),
            )

    def tp_total(which):
        val = tps[which]
        for k in range(1, NX):
            arrived(tpr.at[which, k - 1], t_recv.at[which, k - 1])
            val = val + tpr[which, k - 1]
        return jnp.sqrt(val[:, 0:1]) * lax.rsqrt(val[:, 64:65] + 1e-06)

    for dy in range(NY):
        for dc in range(NC):
            if dy or dc:
                cs = lax.rem(c + dc, NC)
                arrived(gr.at[cs, dy], g_recv.at[dy, dc])
    for h in (0, 1):
        sd[:, pl.ds(512 * h, 512)] = (gr[h, 0] + gr[h, 1] + gr[h, 2] + gr[h, 3]) * 0.125
    tp_send(1, sd[...], md[...])

    for h in (0, 1):
        rows = pl.ds(8 * h, 8)
        val = sum_u[z, rows]
        for direction in (0, 1):
            i = 6 if half_of(direction, 0) == h else 5
            arrived(zr.at[direction, i], z_recv.at[direction, i])
            val = val + zr[direction, i]
        su[rows] = val * 0.125
    tp_send(0, su[...], mu[...])

    stepped, state = updated(md[...], vd[...], sd[...] * tp_total(1))
    sd[...] = stepped
    qd[...] = state
    turned = stepped.astype(BF16)
    gds[0] = turned[:, :512]
    gds[1] = turned[:, 512:]
    for dy in range(NY):
        for dc in range(NC):
            if dy or dc:
                yt, ct = yo(dy), lax.rem(c + dc, NC)
                started(gds.at[ct], gd.at[y, c], gd_send.at[0], gd_recv.at[dy, dc], dp_1=yt, dp_2=ct)
    gd[y, c] = gds[c]

    stepped, state = updated(mu[...], vu[...], su[...] * tp_total(0))
    su[...] = stepped
    qu[...] = state
    out_u[z, y, c] = stepped.astype(BF16)

    lanes = lambda h: pl.ds(512 * h, 512)

    def to_partner_u(zt, yt):
        piece = out_u.at[zt, yt, c]
        started(piece, piece, pair_send.at[0], pair_recv.at[0], dp_2=o)

    def to_y(kz):
        for direction in (0, 1):
            piece = out_u.at[zo(kz), y, c]
            started(
                piece, piece, agy_send.at[direction], agy_recv.at[direction, 0, kz % NZ], dp_1=yo(sign(direction))
            )
        to_partner_u(zo(kz), y)

    def to_z(direction, k):
        s = sign(direction)
        piece = out_u.at[zo(-s * k), y, c]
        if k == 3:
            piece = piece.at[:, lanes(half_of(direction, 0))]
        started(piece, piece, agz_send.at[direction], agz_recv.at[direction, k], dp_0=zo(s))

    def z_came(direction, k):
        piece = out_u.at[zo(-sign(direction) * k), y, c]
        if k == 4:
            piece = piece.at[:, lanes(half_of(direction, 0))]
        arrived(piece, agz_recv.at[direction, k - 1])

    def y_came(kz):
        for direction in (0, 1):
            s = sign(direction)
            piece = out_u.at[zo(kz), yo(-s), c]
            arrived(piece, agy_recv.at[direction, 0, kz % NZ])
            half = piece.at[:, lanes(direction)]
            started(half, half, agy_send.at[direction], agy_recv.at[direction, 1, kz % NZ], dp_1=yo(s))
            to_partner_u(zo(kz), yo(-s))

    def y_far(kz):
        for direction in (0, 1):
            half = out_u.at[zo(kz), yo(2), c].at[:, lanes(direction)]
            arrived(half, agy_recv.at[direction, 1, kz % NZ])
        to_partner_u(zo(kz), yo(2))

    def d_block(kz, h):
        return out_d.at[pl.ds(pl.multiple_of(c * 512 + h * 256, 256), 256), col(zo(kz))]

    def to_dz(direction, k, h):
        block = d_block(-sign(direction) * k, h)
        started(block, block, agd_send.at[direction], agd_recv.at[direction, k, h], dp_0=zo(sign(direction)))

    def to_partner_d(kz, h):
        block = d_block(kz, h)
        started(block, block, pair_send.at[1], pair_recv.at[1], dp_2=o)

    def turn():
        for dy in range(NY):
            for dc in range(NC):
                if dy or dc:
                    arrived(gd.at[yo(-dy), lax.rem(c + dc, NC)], gd_recv.at[dy, dc])
        for b in range(4):
            block = gd[:, :, :, 128 * b : 128 * b + 128].reshape(128, 128).astype(F32)
            out_d[pl.ds(pl.multiple_of(c * 512 + b * 128, 128), 128), col(z)] = block.T.astype(BF16)
        for h in (0, 1):
            for direction in (0, 1):
                to_dz(direction, 0, half_of(direction, h))
        for h in (0, 1):
            to_partner_d(0, h)

    def d_came(k, h):
        for direction in (0, 1):
            hh = half_of(direction, h)
            if k == 4 and h == 1:
                continue
            arrived(d_block(-sign(direction) * k, hh), agd_recv.at[direction, k - 1, hh])
            if k < 3 or (k == 3 and h == 0):
                to_dz(direction, k, hh)
            to_partner_d(-sign(direction) * k, hh)

    def first_u():
        for direction in (0, 1):
            to_z(direction, 0)
        to_y(0)

    def u_came(k):
        for direction in (0, 1):
            z_came(direction, k)
            if k < 4:
                to_z(direction, k)
        if k < 4:
            for direction in (0, 1):
                to_y(-sign(direction) * k)
        else:
            to_y(4)

    first_u()
    turn()
    u_came(1)
    y_came(0)
    d_came(1, 0)
    u_came(2)
    for kz in (-1, 1):
        y_came(kz)
    y_far(0)
    d_came(1, 1)
    u_came(3)
    for kz in (-2, 2):
        y_came(kz)
    for kz in (-1, 1):
        y_far(kz)
    d_came(2, 0)
    u_came(4)
    for kz in (-3, 3):
        y_came(kz)
    d_came(2, 1)
    for kz in (-2, 2):
        y_far(kz)
    y_came(4)
    d_came(3, 0)
    for kz in (-3, 3):
        y_far(kz)
    d_came(3, 1)
    y_far(4)
    d_came(4, 0)

    for yt in range(NY):
        pass
    arrived(out_u.at[:, :, o], pair_recv.at[0])
    arrived(out_d.at[pl.ds(pl.multiple_of(o * 512, 512), 512)], pair_recv.at[1])

    def left(ref, sem):
        pltpu.make_async_copy(ref, ref, sem).wait()

    left(pr_d, s0_send.at[0])
    left(pr_u, s0_send.at[1])
    left(smr.at[0], sm_send.at[0])
    left(smr.at[pl.ds(0, 3)], sm_send.at[1])
    left(smr.at[pl.ds(0, 7)], sm_send.at[2])
    left(gs.at[pl.ds(0, 7)], g_send.at[0])
    left(own_d.at[0, pl.ds(0, 448)], gd_send.at[0])
    left(out_u.at[:, :, c], pair_send.at[0])
    left(out_d.at[pl.ds(pl.multiple_of(c * 512, 512), 512)], pair_send.at[1])
    for direction in (0, 1):
        left(ds.at[direction], d_send.at[direction])
        left(us.at[direction], u_send.at[direction])
        left(zs.at[direction], z_send.at[direction])
        left(tpr.at[direction], t_send.at[direction])
        left(own_d.at[0, pl.ds(0, 448)], agz_send.at[direction])
        left(own_d.at[pl.ds(0, 3)], agy_send.at[direction])
        left(own_d.at[pl.ds(0, 7), pl.ds(0, 256)], agd_send.at[direction])


def local(pu, pd, pn, mu, md, mn, vu, vd, vn):
    place = lax.axis_index(DP)
    mine = (jnp.arange(1024) // 16 == place).reshape(8, 128)
    placed = lambda v: jnp.where(mine, jnp.tile(v, 64).reshape(8, 128), 0.0)
    small = jnp.concatenate([pn.reshape(8, 128).astype(F32), placed(mn), placed(vn)], axis=0)

    vm = pl.BlockSpec(memory_space=pltpu.VMEM)
    hbm = pl.BlockSpec(memory_space=pl.ANY)
    sds = jax.ShapeDtypeStruct
    dma = pltpu.SemaphoreType.DMA
    half = sds((16, 1024), F32)
    out = pl.pallas_call(
        kernel,
        out_shape=(
            sds((NZ, NY, NC, 16, 1024), BF16), sds((1024, 1024), BF16), sds((16, 128), F32), half, half, half, half,
        ),
        in_specs=[vm, hbm, hbm, vm, vm, vm, vm],
        out_specs=(vm,) * 7,
        scratch_shapes=[
            pltpu.VMEM((NZ, NY, 16, 1024), BF16),
            pltpu.VMEM((NZ, NY, 16, 1024), BF16),
            pltpu.VMEM((NZ, 512, 128), BF16),
            pltpu.VMEM((NZ, 512, 128), BF16),
            pltpu.VMEM((2, 7, 256, 128), F32),
            pltpu.VMEM((2, 7, 256, 128), F32),
            pltpu.VMEM((2, 3, 4, 16, 1024), F32),
            pltpu.VMEM((2, 3, 4, 16, 1024), F32),
            pltpu.VMEM((NZ, 16, 1024), F32),
            pltpu.VMEM((2, 7, 8, 1024), F32),
            pltpu.VMEM((2, 7, 8, 1024), F32),
            pltpu.VMEM((8, 16, 512), F32),
            pltpu.VMEM((2, 4, 16, 512), F32),
            pltpu.VMEM((2, 16, 128), F32),
            pltpu.VMEM((2, 3, 16, 128), F32),
            pltpu.VMEM((2, 16, 512), BF16),
            pltpu.VMEM((4, 2, 16, 512), BF16),
            pltpu.VMEM((2, 24, 128), F32),
            pltpu.VMEM((11, 24, 128), F32),
            dma((4,)), dma((8,)), dma((2,)), dma((4,)), dma((8,)),
            dma((2,)), dma((2, 7)), dma((2,)), dma((2, 3)), dma((2,)), dma((2, 7)),
            dma((1,)), dma((4, 2)), dma((2,)), dma((2, 3)), dma((3,)), dma((11,)),
            dma((2,)), dma((2, 4)), dma((2,)), dma((2, 2, 8)), dma((2,)), dma((2, 4, 2)),
            dma((1,)), dma((4, 2)), dma((2,)), dma((2,)),
        ],
        compiler_params=pltpu.CompilerParams(collective_id=0, has_side_effects=True),
        name="update",
    )(small, pu.reshape(NZ, NY, NC, 16, 1024), pd.reshape(2, 512, 1024), mu, md.T, vu, vd.T)
    out_u, out_d, nout, su, sd, qu, qd = out
    own = lambda t: lax.dynamic_slice_in_dim(t.reshape(1024), place * 16, 16)
    return (
        out_u.reshape(1024, 1024), out_d, nout[0:8].reshape(1024).astype(BF16),
        su, sd.T, own(nout[0:8]), qu, qd.T, own(nout[8:16]),
    )


def solution(mesh):
    finer = Mesh(mesh.devices.reshape(NZ, NY, NC, mesh.shape["tp"]), (*DP, "tp"))
    return jax.shard_map(
        local,
        mesh=finer,
        in_specs=(
            P(DP, None, "tp"), P(DP, "tp", None), P(DP, None),
            P(DP, "tp"), P("tp", DP), P(DP),
            P(DP, "tp"), P("tp", DP), P(DP),
        ),
        out_specs=(
            P(None, "tp"), P("tp", None), P(),
            P(DP, "tp"), P("tp", DP), P(DP),
            P(DP, "tp"), P("tp", DP), P(DP),
        ),
        check_vma=False,
    )
```

time: 301 us -> 95 us (0.32)
  waiting for transfers between devices: 201 us -> 0 us
  Pallas kernels: 0 us -> 81.1 us
  blocking collectives: 34.4 us -> 0 us
  local copies, waits for them, and re-layouts: 36 us -> 11.7 us
  between operations: 14.1 us -> 0.68 us
  other arithmetic: 9.73 us -> 1.31 us
  starting transfers between devices: 4.42 us -> 0 us
    reduce_scatter x1 -> x0, waiting for transfers between devices: 116 us -> none  [sum_packed(): lax.psum_scatter(lines, axis, tiled=True).reshape(-1)]
    all_gather x1 -> x0, waiting for transfers between devices: 82 us -> none  [turned_gather(): filled = lax.all_gather(both, axis, axis=0, tiled=True)]
    pallas_call x0 -> x1, Pallas kernels: none -> 81.1 us  [local(): pl.pallas_call(kernel, out_shape=(sds((NZ, NY, NC, 16, 1024), BF16), sds(...]
    psum x3 -> x0, blocking collectives: 34.4 us -> none  [over_axes(): array = lax.psum(array, axis)]
    reshape x6 -> x1, local copies, waits for them, and re-layouts: 13.3 us -> 0.69 us  [local(): own = lambda t: lax.dynamic_slice_in_dim(t.reshape(1024), place * 16, 16)]
    transpose x2 -> x0, local copies, waits for them, and re-layouts: 10.1 us -> none  [the longest x1 6.13 us: cut_along(): return jnp.moveaxis(array.reshape(*before, size, -1, *after), dim, 0)]
    reshape x2 -> x0, other arithmetic: 5.95 us -> none  [the longest x1 5.35 us: sum_packed(): jnp.pad(lines, ((0, 0), (0, width * 128 - lines.shape[1]))).reshape(-1, 128)]
    all_to_all x1 -> x0, starting transfers between devices: 4.38 us -> none  [sent_to_all(): return lax.all_to_all(copies, axis, split_axis=0, concat_axis=0, tiled=True)]
  transfers between devices with their start and end apart: 3 -> 0, of which waited for: 3 -> 0; matrix products, arithmetic and copies ran while one was open for 0% -> 0% of each run, Pallas kernels for 0% -> 0%
where the time goes in v1:
time: 95 us; the launch traced here: 94.8 us
  Pallas kernels  81.1 us (85%)
  local copies, waits for them, and re-layouts  11.7 us (12%)
  other arithmetic  1.31 us (1%)
    pallas_call x1, Pallas kernels, local(): pl.pallas_call(kernel, out_shape=(sds((NZ, NY, NC, 16, 1024), BF16), sds(...  81.1 us
    unnamed x16, local copies, waits for them, and re-layouts  7.09 us

profile of v1, /device:TPU:1, one launch (start us, length us, event | category | flops | bytes accessed | tf_op | source)
XLA Modules:
  0.0 94.8 jit_solution(12653123816919480052)
XLA Ops:
  0.7 0.7 tile.20
  1.3 0.1 tile.21
  1.4 0.7 tile.23
  2.0 0.1 tile.24
  2.1 0.7 convert_element_type.12
  2.8 0.6 pad_maximum_fusion.small
  3.4 81.1 %update.1 = (bf16[8,4,2,16,1024]{4,3,2,1,0:T(8,128)(2,1)}, bf16[1024,1024]{1,0:T(8,128)(2,1)}, f32[16,128]{1,0:T(8,128)}, f32[16,1024]{1,0:T(8,128)}, f32[16,102...) custom-call(f32[24,128]{1,0:T(8,128)} %pad_maximum_fusion.small, bf16[8,4,2,16,1024]{4,3,2,1,0:T(8,128)(2,1)} %bitcast.14, ...), custom_call_target="tpu_custom_call" | custom-call | tf_op jit(solution)/shard_map/update/pallas_call | solution.py:442
  84.5 0.7 slice_bitcast_fusion
  85.2 0.6 dynamic_slice.6
  85.8 0.6 dynamic_slice.7
  86.4 1.3 %fusion.4 = bf16[1024]{0:T(1024)(128)(2,1)} fusion(f32[16,128]{1,0:T(8,128)} %get-tuple-element.18), kind=kLoop, calls=%fused_computation.15 | loop fusion | bytes 4096 | tf_op jit(solution)/shard_map/convert_element_type | solution.py:481
  87.7 0.0 copy-start
  87.7 3.2 %copy.24 = bf16[1024,1024]{1,0:T(8,128)(2,1)} copy(bf16[1024,1024]{1,0:T(8,128)(2,1)} %bitcast.16) | data formatting | bytes 4194304
  90.9 0.0 copy-done
  90.9 0.0 copy-start.4
  90.9 0.0 copy-start.3
  90.9 0.0 copy-start.2
  90.9 0.0 copy-start.1
  90.9 1.3 %copy.25 = bf16[1024,1024]{1,0:T(8,128)(2,1)} copy(bf16[1024,1024]{1,0:T(8,128)(2,1)S(1)} %copy-done) | data formatting | bytes 4194304
  92.2 0.0 copy-done.4
  92.2 0.6 copy.26
  92.9 0.0 copy-done.3
  92.9 0.6 copy.27
  93.5 0.0 copy-done.2
  93.5 0.6 copy.28
  94.1 0.0 copy-done.1
  94.1 0.6 copy.29
  (1 shorter events, 0.0 us)
Async XLA Ops:
  87.7 3.2 %copy-start = (bf16[1024,1024]{1,0:T(8,128)(2,1)S(1)}, bf16[1024,1024]{1,0:T(8,128)(2,1)}, u32[]{:S(2)}) copy-start(bf16[1024,1024]{1,0:T(8,128)(2,1)} %get-tuple-element.37) | copy-start | bytes 6291460
  90.9 1.3 %copy-start.4 = (f32[16,1024]{1,0:T(8,128)S(1)}, f32[16,1024]{1,0:T(8,128)}, u32[]{:S(2)}) copy-start(f32[16,1024]{1,0:T(8,128)} %get-tuple-element.39) | copy-start | bytes 196612
  90.9 2.0 %copy-start.3 = (f32[16,1024]{1,0:T(8,128)S(1)}, f32[16,1024]{1,0:T(8,128)}, u32[]{:S(2)}) copy-start(f32[16,1024]{1,0:T(8,128)} %get-tuple-element.20) | copy-start | bytes 196612
  90.9 2.6 %copy-start.2 = (f32[16,1024]{1,0:T(8,128)S(1)}, f32[16,1024]{1,0:T(8,128)}, u32[]{:S(2)}) copy-start(f32[16,1024]{1,0:T(8,128)} %get-tuple-element.42) | copy-start | bytes 196612
  90.9 3.2 %copy-start.1 = (f32[16,1024]{1,0:T(8,128)S(1)}, f32[16,1024]{1,0:T(8,128)}, u32[]{:S(2)}) copy-start(f32[16,1024]{1,0:T(8,128)} %get-tuple-element.22) | copy-start | bytes 196612

commit v2 on v1

--- a/solution.py
+++ b/solution.py
@@ -16,6 +16,8 @@
 learn_rate = 0.025
 hold_rate = 0.8
 
+VMEM_LIMIT = int(49 * 2**20)
+
 
 def updated(master, memory, mean):
     state = hold_rate * memory + (1.0 - hold_rate) * mean * mean
@@ -30,10 +32,10 @@
 
 
 def kernel(
-    small, pu, pd, mu, md, vu, vd,
-    out_u, out_d, nout, su, sd, qu, qd,
-    own_u, pr_u, own_d, pr_d, ds, dr, us, ur, sum_u, zs, zr, gs, gr, tps, tpr, gds, gd, sms, smr,
-    loc_u, loc_d, s0_send, s0u_recv, s0d_recv, d_send, d_recv, u_send, u_recv, z_send, z_recv,
+    own, pu_in, pd_in,
+    out_u, out_d, state_out, nout,
+    pu, pd, pr_u, pr_d, ds, dr, us, ur, sum_u, zs, zr, gs, gr, tps, tpr, gds, gd, sms, smr, rolled, su, sd,
+    loc, s0_send, s0u_recv, s0d_recv, d_send, d_recv, u_send, u_recv, z_send, z_recv,
     g_send, g_recv, t_send, t_recv, sm_send, sm_recv,
     agz_send, agz_recv, agy_send, agy_recv, agd_send, agd_recv, gd_send, gd_recv, pair_send, pair_recv,
 ):
@@ -57,26 +59,47 @@
     zorder = (4, 3, -3, 2, -2, 1, -1, 0)
     yorder = (2, 1, -1, 0)
     col = lambda zt: pl.ds(pl.multiple_of(zt * 128, 128), 128)
-    for i, k in enumerate(zorder):
-        pltpu.make_async_copy(pd.at[c, :, col(zo(k))], own_d.at[zo(k)], loc_d.at[i]).start()
-    for i, k in enumerate(yorder):
-        pltpu.make_async_copy(pu.at[:, yo(k), c], own_u.at[:, yo(k)], loc_u.at[i]).start()
+
+    pltpu.make_async_copy(pd_in, pd, loc.at[0]).start()
+    pltpu.make_async_copy(pu_in, pu, loc.at[1]).start()
+    mu, md, vu, vd = (own.at[pl.ds(16 * i, 16)] for i in range(4))
+
+    spread = lax.rem(16 * (y * NC + c), 128)
+    row = own[64:72]
+    for i in range(8):
+        sms[0, i : i + 1] = row[0:1, 128 * i : 128 * i + 128]
+    sms[0, 8:24] = jnp.zeros((16, 128), F32)
+    for i in (0, 1):
+        rolled[i] = jnp.broadcast_to(row[i + 1 : i + 2, 0:128], (8, 128))
+        sms[0, pl.ds(8 + 8 * i + z, 1)] = pltpu.roll(rolled[i], spread, 1)[0:1]
 
     barrier = pltpu.get_barrier_semaphore()
-    peers = [{"dp_0": zo(k)} for k in range(1, NZ)]
+    peers = [{"dp_0": zo(k)} for k in (1, -1, 2, -2)]
     peers += [{"dp_1": yo(dy), "dp_2": lax.rem(c + dc, NC)} for dy in range(NY) for dc in range(NC) if dy or dc]
     peers += [{"tp": lax.rem(x + k, NX)} for k in range(1, NX)]
     for dev in peers:
         pl.semaphore_signal(barrier, inc=1, device_id=dev, device_id_type=MESH)
     pl.semaphore_wait(barrier, len(peers))
 
-    for i in range(8):
-        zt = zo(zorder[i])
-        started(pd.at[o, :, col(zt)], pr_d.at[zt], s0_send.at[0], s0d_recv.at[i], dp_2=o)
-        if i % 2 == 0:
-            yt = yo(yorder[i // 2])
-            started(pu.at[:, yt, o], pr_u.at[:, yt], s0_send.at[1], s0u_recv.at[i // 2], dp_2=o)
-    started(small, smr.at[0], sm_send.at[0], sm_recv.at[0], dp_2=o)
+    pltpu.make_async_copy(pd_in, pd, loc.at[0]).wait()
+    pltpu.make_async_copy(pu_in, pu, loc.at[1]).wait()
+
+    def pair_d(*ks):
+        for k in ks:
+            started(
+                pd.at[o, :, col(zo(k))], pr_d.at[zo(k)], s0_send.at[0], s0d_recv.at[zorder.index(k)], dp_2=o
+            )
+
+    def pair_u(*ks):
+        for k in ks:
+            started(
+                pu.at[:, yo(k), o], pr_u.at[:, yo(k)], s0_send.at[1], s0u_recv.at[yorder.index(k)], dp_2=o
+            )
+
+    pair_d(4)
+    pair_u(2)
+    pair_d(3, -3)
+    pair_u(1, -1)
 
     have = set()
 
@@ -84,14 +107,12 @@
         if ("d", k) not in have:
             have.add(("d", k))
             i = zorder.index(k)
-            pltpu.make_async_copy(pd.at[c, :, col(zo(k))], own_d.at[zo(k)], loc_d.at[i]).wait()
             arrived(pr_d.at[zo(k)], s0d_recv.at[i])
 
     def need_u(k):
         if ("u", k) not in have:
             have.add(("u", k))
             i = yorder.index(k)
-            pltpu.make_async_copy(pu.at[:, yo(k), c], own_u.at[:, yo(k)], loc_u.at[i]).wait()
             arrived(pr_u.at[:, yo(k)], s0u_recv.at[i])
 
     zslots, yslots = slots_of(NZ), slots_of(NY)
@@ -108,7 +129,7 @@
         kk = 4 if k == -4 else k
         need_d(kk)
         rows = pl.ds(half_of(direction, h) * 256, 256)
-        val = own_d[zo(kk), rows].astype(F32) + pr_d[zo(kk), rows].astype(F32)
+        val = pd[c, rows, col(zo(kk))].astype(F32) + pr_d[zo(kk), rows].astype(F32)
         if i >= 2:
             arrived(dr.at[direction, i - 2], d_recv.at[direction, i - 2])
             val = val + dr[direction, i - 2]
@@ -124,7 +145,7 @@
         kk = 2 if k == -2 else k
         need_u(kk)
         part = pl.ds(half_of(direction, h) * 4, 4)
-        val = own_u[part, yo(kk)].astype(F32) + pr_u[part, yo(kk)].astype(F32)
+        val = pu[part, yo(kk), c].astype(F32) + pr_u[part, yo(kk)].astype(F32)
         if i >= 2:
             arrived(ur.at[direction, i - 2], u_recv.at[direction, i - 2])
             val = val + ur[direction, i - 2]
@@ -154,42 +175,38 @@
         for direction in (0, 1):
             u_slot(direction, i)
 
-    arrived(smr.at[0], sm_recv.at[0])
-    sms[0] = small[...] + smr[0]
-    for dy in range(1, NY):
-        started(sms.at[0], smr.at[dy], sm_send.at[1], sm_recv.at[dy], dp_1=yo(dy))
-
-    for direction in (0, 1):
-        d_slot(direction, 2)
-    for direction in (0, 1):
-        d_slot(direction, 3)
+    pair_d(2, -2, 1, -1)
+    started(sms.at[0], smr.at[0], sm_send.at[0], sm_recv.at[0], dp_2=o)
+    pair_d(0)
+    pair_u(0)
+    for i in (2, 3):
+        for direction in (0, 1):
+            d_slot(direction, i)
     for direction in (0, 1):
         u_slot(direction, 2)
 
-    total = sms[0]
+    arrived(smr.at[0], sm_recv.at[0])
+    sms[1] = sms[0] + smr[0]
     for dy in range(1, NY):
-        arrived(smr.at[dy], sm_recv.at[dy])
-        total = total + smr[dy]
-    sms[1] = total
-    for k in range(1, NZ):
-        started(sms.at[1], smr.at[3 + k], sm_send.at[2], sm_recv.at[3 + k], dp_0=zo(k))
+        started(sms.at[1], smr.at[dy], sm_send.at[1], sm_recv.at[dy], dp_1=yo(dy))
+
+    def norm_on(k):
+        for direction in (0, 1):
+            if 0 < k <= 4 - direction:
+                arrived(smr.at[3 + 4 * direction + k], sm_recv.at[3 + 4 * direction + k])
+            if k < 4 - direction:
+                src = smr.at[3 + 4 * direction + k] if k else sms.at[2]
+                i = 4 + 4 * direction + k
+                started(src, smr.at[i], sm_send.at[2 + direction], sm_recv.at[i], dp_0=zo(sign(direction)))
 
     for i in (4, 5, 6):
         for direction in (0, 1):
             d_slot(direction, i)
-
-    total = sms[1]
-    for k in range(1, NZ):
-        arrived(smr.at[3 + k], sm_recv.at[3 + k])
-        total = total + smr[3 + k]
-    stepped, state = updated(total[8:16], total[16:24], total[0:8] * 0.125)
-    nout[0:8] = stepped
-    nout[8:16] = state
 
     need_u(0)
     for h in (0, 1):
         part = pl.ds(4 * h, 4)
-        val = own_u[part, y].astype(F32) + pr_u[part, y].astype(F32)
+        val = pu[part, y, c].astype(F32) + pr_u[part, y].astype(F32)
         for direction in (0, 1):
             i = 2 if half_of(direction, 0) == h else 1
             arrived(ur.at[direction, i], u_recv.at[direction, i])
@@ -199,10 +216,17 @@
         for direction in (0, 1):
             z_slot(direction, i)
 
+    total = sms[1]
+    for dy in range(1, NY):
+        arrived(smr.at[dy], sm_recv.at[dy])
+        total = total + smr[dy]
+    sms[2] = total
+    norm_on(0)
+
     need_d(0)
     for h in (0, 1):
         rows = pl.ds(256 * h, 256)
-        val = own_d[z, rows].astype(F32) + pr_d[z, rows].astype(F32)
+        val = pd[c, rows, col(z)].astype(F32) + pr_d[z, rows].astype(F32)
         for direction in (0, 1):
             i = 6 if half_of(direction, 0) == h else 5
             arrived(dr.at[direction, i], d_recv.at[direction, i])
@@ -218,9 +242,10 @@
                 )
     gr[c, 0] = gs[y * NC + c]
 
-    for i in (2, 3, 4, 5, 6):
-        for direction in (0, 1):
-            z_slot(direction, i)
+    def z_step(*steps):
+        for i in steps:
+            for direction in (0, 1):
+                z_slot(direction, i)
 
     lane = lax.broadcasted_iota(jnp.int32, (16, 128), 1)
 
@@ -241,42 +266,60 @@
             val = val + tpr[which, k - 1]
         return jnp.sqrt(val[:, 0:1]) * lax.rsqrt(val[:, 64:65] + 1e-06)
 
-    for dy in range(NY):
-        for dc in range(NC):
-            if dy or dc:
-                cs = lax.rem(c + dc, NC)
-                arrived(gr.at[cs, dy], g_recv.at[dy, dc])
-    for h in (0, 1):
-        sd[:, pl.ds(512 * h, 512)] = (gr[h, 0] + gr[h, 1] + gr[h, 2] + gr[h, 3]) * 0.125
-    tp_send(1, sd[...], md[...])
-
-    for h in (0, 1):
-        rows = pl.ds(8 * h, 8)
-        val = sum_u[z, rows]
-        for direction in (0, 1):
-            i = 6 if half_of(direction, 0) == h else 5
-            arrived(zr.at[direction, i], z_recv.at[direction, i])
-            val = val + zr[direction, i]
-        su[rows] = val * 0.125
-    tp_send(0, su[...], mu[...])
-
-    stepped, state = updated(md[...], vd[...], sd[...] * tp_total(1))
-    sd[...] = stepped
-    qd[...] = state
-    turned = stepped.astype(BF16)
-    gds[0] = turned[:, :512]
-    gds[1] = turned[:, 512:]
-    for dy in range(NY):
-        for dc in range(NC):
-            if dy or dc:
-                yt, ct = yo(dy), lax.rem(c + dc, NC)
-                started(gds.at[ct], gd.at[y, c], gd_send.at[0], gd_recv.at[dy, dc], dp_1=yt, dp_2=ct)
-    gd[y, c] = gds[c]
-
-    stepped, state = updated(mu[...], vu[...], su[...] * tp_total(0))
-    su[...] = stepped
-    qu[...] = state
-    out_u[z, y, c] = stepped.astype(BF16)
+    def down_sum():
+        for dy in range(NY):
+            for dc in range(NC):
+                if dy or dc:
+                    cs = lax.rem(c + dc, NC)
+                    arrived(gr.at[cs, dy], g_recv.at[dy, dc])
+        for h in (0, 1):
+            sd[:, pl.ds(512 * h, 512)] = (gr[h, 0] + gr[h, 1] + gr[h, 2] + gr[h, 3]) * 0.125
+        tp_send(1, sd[...], md[...])
+
+    def up_sum():
+        for h in (0, 1):
+            rows = pl.ds(8 * h, 8)
+            val = sum_u[z, rows]
+            for direction in (0, 1):
+                i = 6 if half_of(direction, 0) == h else 5
+                arrived(zr.at[direction, i], z_recv.at[direction, i])
+                val = val + zr[direction, i]
+            su[rows] = val * 0.125
+        tp_send(0, su[...], mu[...])
+
+    def down_update():
+        stepped, state = updated(md[...], vd[...], sd[...] * tp_total(1))
+        state_out[16:32] = stepped
+        state_out[48:64] = state
+        turned = stepped.astype(BF16)
+        gds[0] = turned[:, :512]
+        gds[1] = turned[:, 512:]
+        for dy in range(NY):
+            for dc in range(NC):
+                if dy or dc:
+                    yt, ct = yo(dy), lax.rem(c + dc, NC)
+                    started(gds.at[ct], gd.at[y, c], gd_send.at[0], gd_recv.at[dy, dc], dp_1=yt, dp_2=ct)
+        gd[y, c] = gds[c]
+
+    def up_update():
+        stepped, state = updated(mu[...], vu[...], su[...] * tp_total(0))
+        state_out[0:16] = stepped
+        state_out[32:48] = state
+        out_u[z, y, c] = stepped.astype(BF16)
+
+    def norm_update():
+        total = sms[2]
+        for k in range(7):
+            total = total + smr[4 + k]
+        stepped, state = updated(total[8:16], total[16:24], total[0:8] * 0.125)
+        rolled[0] = stepped
+        rolled[1] = state
+        for i in range(8):
+            nout[0:1, 128 * i : 128 * i + 128] = stepped[i : i + 1]
+        back = lax.rem(128 - spread, 128)
+        for i in (0, 1):
+            mine = jnp.broadcast_to(rolled[i, pl.ds(z, 1)], (8, 128))
+            nout[8 + 8 * i : 16 + 8 * i, 0:128] = pltpu.roll(mine, back, 1)
 
     lanes = lambda h: pl.ds(512 * h, 512)
 
@@ -295,9 +338,10 @@
     def to_z(direction, k):
         s = sign(direction)
         piece = out_u.at[zo(-s * k), y, c]
-        if k == 3:
+        started(piece, piece, agz_send.at[direction], agz_recv.at[direction, k], dp_0=zo(s))
+        if k:
             piece = piece.at[:, lanes(half_of(direction, 0))]
-        started(piece, piece, agz_send.at[direction], agz_recv.at[direction, k], dp_0=zo(s))
+        started(piece, piece, agz_send.at[direction], agz_recv.at[direction, k + 1], dp_0=zo(2 * s))
 
     def z_came(direction, k):
         piece = out_u.at[zo(-sign(direction) * k), y, c]
@@ -363,7 +407,7 @@
     def u_came(k):
         for direction in (0, 1):
             z_came(direction, k)
-            if k < 4:
+            if k == 2:
                 to_z(direction, k)
         if k < 4:
             for direction in (0, 1):
@@ -371,38 +415,48 @@
         else:
             to_y(4)
 
+    z_step(2, 3)
+    norm_on(1)
+    down_sum()
+    z_step(4)
+    down_update()
+    z_step(5, 6)
+    turn()
+    up_sum()
+    norm_on(2)
+    d_came(1, 0)
+    up_update()
     first_u()
-    turn()
+    d_came(1, 1)
+    d_came(2, 0)
+    y_came(0)
     u_came(1)
-    y_came(0)
-    d_came(1, 0)
+    norm_on(3)
+    d_came(2, 1)
     u_came(2)
+    y_far(0)
     for kz in (-1, 1):
         y_came(kz)
-    y_far(0)
-    d_came(1, 1)
+    d_came(3, 0)
+    d_came(3, 1)
+    norm_on(4)
+    norm_update()
     u_came(3)
+    for kz in (-1, 1):
+        y_far(kz)
     for kz in (-2, 2):
         y_came(kz)
-    for kz in (-1, 1):
+    d_came(4, 0)
+    u_came(4)
+    for kz in (-2, 2):
         y_far(kz)
-    d_came(2, 0)
-    u_came(4)
     for kz in (-3, 3):
         y_came(kz)
-    d_came(2, 1)
-    for kz in (-2, 2):
-        y_far(kz)
     y_came(4)
-    d_came(3, 0)
     for kz in (-3, 3):
         y_far(kz)
-    d_came(3, 1)
     y_far(4)
-    d_came(4, 0)
-
-    for yt in range(NY):
-        pass
+
     arrived(out_u.at[:, :, o], pair_recv.at[0])
     arrived(out_d.at[pl.ds(pl.multiple_of(o * 512, 512), 512)], pair_recv.at[1])
 
@@ -413,9 +467,10 @@
     left(pr_u, s0_send.at[1])
     left(smr.at[0], sm_send.at[0])
     left(smr.at[pl.ds(0, 3)], sm_send.at[1])
-    left(smr.at[pl.ds(0, 7)], sm_send.at[2])
+    left(smr.at[pl.ds(0, 4)], sm_send.at[2])
+    left(smr.at[pl.ds(0, 3)], sm_send.at[3])
     left(gs.at[pl.ds(0, 7)], g_send.at[0])
-    left(own_d.at[0, pl.ds(0, 448)], gd_send.at[0])
+    left(pr_d.at[0, pl.ds(0, 448)], gd_send.at[0])
     left(out_u.at[:, :, c], pair_send.at[0])
     left(out_d.at[pl.ds(pl.multiple_of(c * 512, 512), 512)], pair_send.at[1])
     for direction in (0, 1):
@@ -423,33 +478,38 @@
         left(us.at[direction], u_send.at[direction])
         left(zs.at[direction], z_send.at[direction])
         left(tpr.at[direction], t_send.at[direction])
-        left(own_d.at[0, pl.ds(0, 448)], agz_send.at[direction])
-        left(own_d.at[pl.ds(0, 3)], agy_send.at[direction])
-        left(own_d.at[pl.ds(0, 7), pl.ds(0, 256)], agd_send.at[direction])
+        left(pr_d.at[0, pl.ds(0, 448)], agz_send.at[direction])
+        left(pr_d.at[pl.ds(0, 3)], agy_send.at[direction])
+        left(pr_d.at[pl.ds(0, 7), pl.ds(0, 256)], agd_send.at[direction])
+
+
+def finish(cu, cd, st, cu_out, cd_out, su, sd, qu, qd, sem):
+    copies = [pltpu.make_async_copy(cu, cu_out, sem.at[0]), pltpu.make_async_copy(cd, cd_out, sem.at[1])]
+    for i, ref in enumerate((su, sd, qu, qd)):
+        copies.append(pltpu.make_async_copy(st.at[pl.ds(16 * i, 16)], ref, sem.at[2 + i]))
+    for copy in copies:
+        copy.start()
+    for copy in copies:
+        copy.wait()
 
 
 def local(pu, pd, pn, mu, md, mn, vu, vd, vn):
-    place = lax.axis_index(DP)
-    mine = (jnp.arange(1024) // 16 == place).reshape(8, 128)
-    placed = lambda v: jnp.where(mine, jnp.tile(v, 64).reshape(8, 128), 0.0)
-    small = jnp.concatenate([pn.reshape(8, 128).astype(F32), placed(mn), placed(vn)], axis=0)
-
     vm = pl.BlockSpec(memory_space=pltpu.VMEM)
     hbm = pl.BlockSpec(memory_space=pl.ANY)
     sds = jax.ShapeDtypeStruct
     dma = pltpu.SemaphoreType.DMA
-    half = sds((16, 1024), F32)
-    out = pl.pallas_call(
+    wide = lambda v: jnp.pad(v.reshape(1, 16), ((0, 0), (0, 1008)))
+    own = jnp.concatenate([mu, md.T, vu, vd.T, pn.astype(F32), wide(mn), wide(vn), jnp.zeros((5, 1024), F32)], axis=0)
+    up, down, state = sds((NZ, NY, NC, 16, 1024), BF16), sds((1024, 1024), BF16), sds((16, 1024), F32)
+    out_u, out_d, states, nout = pl.pallas_call(
         kernel,
-        out_shape=(
-            sds((NZ, NY, NC, 16, 1024), BF16), sds((1024, 1024), BF16), sds((16, 128), F32), half, half, half, half,
-        ),
-        in_specs=[vm, hbm, hbm, vm, vm, vm, vm],
-        out_specs=(vm,) * 7,
+        out_shape=(up, down, sds((64, 1024), F32), sds((24, 1024), F32)),
+        in_specs=[vm, hbm, hbm],
+        out_specs=(vm,) * 4,
         scratch_shapes=[
+            pltpu.VMEM((NZ, NY, NC, 16, 1024), BF16),
+            pltpu.VMEM((2, 512, 1024), BF16),
             pltpu.VMEM((NZ, NY, 16, 1024), BF16),
-            pltpu.VMEM((NZ, NY, 16, 1024), BF16),
-            pltpu.VMEM((NZ, 512, 128), BF16),
             pltpu.VMEM((NZ, 512, 128), BF16),
             pltpu.VMEM((2, 7, 256, 128), F32),
             pltpu.VMEM((2, 7, 256, 128), F32),
@@ -464,22 +524,34 @@
             pltpu.VMEM((2, 3, 16, 128), F32),
             pltpu.VMEM((2, 16, 512), BF16),
             pltpu.VMEM((4, 2, 16, 512), BF16),
-            pltpu.VMEM((2, 24, 128), F32),
+            pltpu.VMEM((3, 24, 128), F32),
             pltpu.VMEM((11, 24, 128), F32),
-            dma((4,)), dma((8,)), dma((2,)), dma((4,)), dma((8,)),
+            pltpu.VMEM((2, 8, 128), F32),
+            pltpu.VMEM((16, 1024), F32),
+            pltpu.VMEM((16, 1024), F32),
+            dma((2,)), dma((2,)), dma((4,)), dma((8,)),
             dma((2,)), dma((2, 7)), dma((2,)), dma((2, 3)), dma((2,)), dma((2, 7)),
-            dma((1,)), dma((4, 2)), dma((2,)), dma((2, 3)), dma((3,)), dma((11,)),
+            dma((1,)), dma((4, 2)), dma((2,)), dma((2, 3)), dma((4,)), dma((11,)),
             dma((2,)), dma((2, 4)), dma((2,)), dma((2, 2, 8)), dma((2,)), dma((2, 4, 2)),
             dma((1,)), dma((4, 2)), dma((2,)), dma((2,)),
         ],
-        compiler_params=pltpu.CompilerParams(collective_id=0, has_side_effects=True),
+        compiler_params=pltpu.CompilerParams(
+            collective_id=0, has_side_effects=True, vmem_limit_bytes=VMEM_LIMIT
+        ),
         name="update",
-    )(small, pu.reshape(NZ, NY, NC, 16, 1024), pd.reshape(2, 512, 1024), mu, md.T, vu, vd.T)
-    out_u, out_d, nout, su, sd, qu, qd = out
-    own = lambda t: lax.dynamic_slice_in_dim(t.reshape(1024), place * 16, 16)
+    )(own, pu.reshape(NZ, NY, NC, 16, 1024), pd.reshape(2, 512, 1024))
+    cu, cd, su, sd, qu, qd = pl.pallas_call(
+        finish,
+        out_shape=(up, down, state, state, state, state),
+        in_specs=[vm] * 3,
+        out_specs=(hbm,) * 6,
+        scratch_shapes=[dma((6,))],
+        compiler_params=pltpu.CompilerParams(vmem_limit_bytes=2**20),
+        name="finish",
+    )(out_u, out_d, states)
     return (
-        out_u.reshape(1024, 1024), out_d, nout[0:8].reshape(1024).astype(BF16),
-        su, sd.T, own(nout[0:8]), qu, qd.T, own(nout[8:16]),
+        cu.reshape(1024, 1024), cd, nout[0].astype(BF16),
+        su, sd.T, nout[8, :16], qu, qd.T, nout[16, :16],
     )
 
 

time: 95 us -> 82.6 us (0.87)
  Pallas kernels: 81.1 us -> 75.1 us
  local copies, waits for them, and re-layouts: 11.7 us -> 6.53 us
  other arithmetic: 1.31 us -> 0 us
    unnamed x16 -> x0, local copies, waits for them, and re-layouts: 7.09 us -> none
    pallas_call x1 -> x2, Pallas kernels: 81.1 us -> 75.1 us  [the longest x1 73 us: local(): pl.pallas_call(kernel, out_shape=(up, down, sds((64, 1024), F32), sds((24...]
    concatenate x0 -> x1, local copies, waits for them, and re-layouts: none -> 4.09 us  [local(): jnp.concatenate([mu, md.T, vu, vd.T, pn.astype(F32), wide(mn), wide(vn),...]
    another operation x4 -> x0, local copies, waits for them, and re-layouts: 1.48 us -> none  [local(): placed = lambda v: jnp.where(mine, jnp.tile(v, 64).reshape(8, 128), 0.0)]
    pad x0 -> x2, local copies, waits for them, and re-layouts: none -> 1.32 us  [local(): wide = lambda v: jnp.pad(v.reshape(1, 16), ((0, 0), (0, 1008)))]
    convert_element_type x1 -> x0, local copies, waits for them, and re-layouts: 1.26 us -> none  [local(): nout[0:8].reshape(1024).astype(BF16)]
    dynamic_slice x2 -> x0, local copies, waits for them, and re-layouts: 1.17 us -> none  [local(): own = lambda t: lax.dynamic_slice_in_dim(t.reshape(1024), place * 16, 16)]
where the time goes in v2:
time: 82.6 us; the launch traced here: 82.3 us
  Pallas kernels  75.1 us (91%)
  local copies, waits for them, and re-layouts  6.53 us (8%)
    pallas_call x1, Pallas kernels, local(): pl.pallas_call(kernel, out_shape=(up, down, sds((64, 1024), F32), sds((24...  73 us
    concatenate x1, local copies, waits for them, and re-layouts, local(): jnp.concatenate([mu, md.T, vu, vd.T, pn.astype(F32), wide(mn), wide(vn),...  4.09 us
    pallas_call x1, Pallas kernels, local(): pl.pallas_call(finish, out_shape=(up, down, state, state, state, state),...  2.12 us

profile of v2, /device:TPU:1, one launch (start us, length us, event | category | flops | bytes accessed | tf_op | source)
XLA Modules:
  0.0 82.3 jit_solution(15808393191408816138)
XLA Ops:
  0.6 0.7 pad.7
  1.3 0.7 pad.8
  2.0 4.1 %concatenate.3.own = f32[72,1024]{1,0:T(8,128)S(1)} concatenate(f32[16,1024]{1,0:T(8,128)} %param.12, f32[16,1024]{1,0:T(8,128)} %bitcast.15, f32[16,1024]{1,0:T(8,128)} %param.15, f32[16,1024]{1,0:T(8,128)} %bitcast.16, bf16[1,1024]{1,0:T(2,128)(2,1)} %param.11, f32[1,1024]{1,0:T(1,128)S(1)} %pad.7, f32[1,1024]{1,0:T(1,128)S(1)} %pad.8, f32[5,1024]{1,0:T(8,128)S(1)} %broadcast_in_dim.3), dimensions={0} | concatenate | bytes 587776 | tf_op jit(solution)/shard_map/concatenate | solution.py:502
  6.1 73.0 %update.1 = (bf16[8,4,2,16,1024]{4,3,2,1,0:T(8,128)(2,1)S(1)}, bf16[1024,1024]{1,0:T(8,128)(2,1)S(1)}, f32[64,1024]{1,0:T(8,128)S(1)}, f32[24,1024]{1,0:T(8,128)S(1)}) custom-call(f32[72,1024]{1,0:T(8,128)S(1)} %concatenate.3.own, bf16[8,4,2,16,1024]{4,3,2,1,0:T(8,128)(2,1)} %bitcast.13, bf16[2,512,1024]{2,1,0:T(8,128)(2,1)} %bitcast.14), custom_call_target="tpu_custom_call" | custom-call | tf_op jit(solution)/shard_map/update/pallas_call | solution.py:504
  79.1 2.1 %finish.1 = (bf16[8,4,2,16,1024]{4,3,2,1,0:T(8,128)(2,1)}, bf16[1024,1024]{1,0:T(8,128)(2,1)}, f32[16,1024]{1,0:T(8,128)}, f32[16,1024]{1,0:T(8,128)}, f32[16,1024]{1,0:T(8,128)}, /*index=5*/f32[16,1024]{1,0:T(8,128)}) custom-call(bf16[8,4,2,16,1024]{4,3,2,1,0:T(8,128)(2,1)S(1)} %get-tuple-element.19.cu, bf16[1024,1024]{1,0:T(8,128)(2,1)S(1)} %get-tuple-element.20.cd, ...), custom_call_target="tpu_custom_call" | custom-call | tf_op jit(solution)/shard_map/finish/pallas_call | solution.py:543
  81.2 0.5 slice_bitcast_fusion
  81.7 0.6 fusion
  (1 shorter events, 0.0 us)

commit v3 on v2

--- a/solution.py
+++ b/solution.py
@@ -16,7 +16,7 @@
 learn_rate = 0.025
 hold_rate = 0.8
 
-VMEM_LIMIT = int(49 * 2**20)
+VMEM_LIMIT = 49 * 2**20
 
 
 def updated(master, memory, mean):
@@ -233,7 +233,7 @@
             val = val + dr[direction, i]
         for b in (0, 1):
             gs[:, :, pl.ds(256 * h + 128 * b, 128)] = val[128 * b : 128 * b + 128].T.reshape(NY * NC, 16, 128)
-    for dy in range(NY):
+    for dy in (2, 1, 3, 0):
         for dc in range(NC):
             if dy or dc:
                 yt, ct = yo(dy), lax.rem(c + dc, NC)
@@ -294,7 +294,7 @@
         turned = stepped.astype(BF16)
         gds[0] = turned[:, :512]
         gds[1] = turned[:, 512:]
-        for dy in range(NY):
+        for dy in (2, 1, 3, 0):
             for dc in range(NC):
                 if dy or dc:
                     yt, ct = yo(dy), lax.rem(c + dc, NC)
@@ -314,12 +314,11 @@
         stepped, state = updated(total[8:16], total[16:24], total[0:8] * 0.125)
         rolled[0] = stepped
         rolled[1] = state
-        for i in range(8):
-            nout[0:1, 128 * i : 128 * i + 128] = stepped[i : i + 1]
+        nout[0:8] = stepped
         back = lax.rem(128 - spread, 128)
         for i in (0, 1):
             mine = jnp.broadcast_to(rolled[i, pl.ds(z, 1)], (8, 128))
-            nout[8 + 8 * i : 16 + 8 * i, 0:128] = pltpu.roll(mine, back, 1)
+            nout[8 + 8 * i : 16 + 8 * i] = pltpu.roll(mine, back, 1)
 
     lanes = lambda h: pl.ds(512 * h, 512)
 
@@ -383,9 +382,12 @@
         for b in range(4):
             block = gd[:, :, :, 128 * b : 128 * b + 128].reshape(128, 128).astype(F32)
             out_d[pl.ds(pl.multiple_of(c * 512 + b * 128, 128), 128), col(z)] = block.T.astype(BF16)
-        for h in (0, 1):
-            for direction in (0, 1):
-                to_dz(direction, 0, half_of(direction, h))
+        for direction in (0, 1):
+            to_dz(direction, 0, half_of(direction, 0))
+
+    def turn_rest():
+        for direction in (0, 1):
+            to_dz(direction, 0, half_of(direction, 1))
         for h in (0, 1):
             to_partner_d(0, h)
 
@@ -418,47 +420,48 @@
     z_step(2, 3)
     norm_on(1)
     down_sum()
-    z_step(4)
+    z_step(4, 5, 6)
     down_update()
-    z_step(5, 6)
-    turn()
     up_sum()
     norm_on(2)
-    d_came(1, 0)
+    turn()
     up_update()
     first_u()
-    d_came(1, 1)
-    d_came(2, 0)
+    turn_rest()
+    d_came(1, 0)
     y_came(0)
     u_came(1)
     norm_on(3)
-    d_came(2, 1)
     u_came(2)
+    d_came(1, 1)
     y_far(0)
+    d_came(2, 0)
     for kz in (-1, 1):
         y_came(kz)
-    d_came(3, 0)
-    d_came(3, 1)
+    u_came(3)
+    for kz in (-2, 2):
+        y_came(kz)
+    d_came(2, 1)
+    u_came(4)
+    for kz in (-1, 1):
+        y_far(kz)
     norm_on(4)
     norm_update()
-    u_came(3)
-    for kz in (-1, 1):
-        y_far(kz)
-    for kz in (-2, 2):
-        y_came(kz)
-    d_came(4, 0)
-    u_came(4)
+    d_came(3, 0)
     for kz in (-2, 2):
         y_far(kz)
-    for kz in (-3, 3):
+    for kz in (-3, 3, 4):
         y_came(kz)
-    y_came(4)
-    for kz in (-3, 3):
+    d_came(3, 1)
+    d_came(4, 0)
+    for kz in (-3, 3, 4):
         y_far(kz)
-    y_far(4)
-
-    arrived(out_u.at[:, :, o], pair_recv.at[0])
-    arrived(out_d.at[pl.ds(pl.multiple_of(o * 512, 512), 512)], pair_recv.at[1])
+
+    def pair_came():
+        arrived(out_u.at[:, :, o], pair_recv.at[0])
+        arrived(out_d.at[pl.ds(pl.multiple_of(o * 512, 512), 512)], pair_recv.at[1])
+
+    pair_came()
 
     def left(ref, sem):
         pltpu.make_async_copy(ref, ref, sem).wait()
@@ -483,12 +486,15 @@
         left(pr_d.at[pl.ds(0, 7), pl.ds(0, 256)], agd_send.at[direction])
 
 
-def finish(cu, cd, st, cu_out, cd_out, su, sd, qu, qd, sem):
+def finish(cu, cd, st, nout, cu_out, cd_out, su, sd, qu, qd, cn, sn, qn, sem):
     copies = [pltpu.make_async_copy(cu, cu_out, sem.at[0]), pltpu.make_async_copy(cd, cd_out, sem.at[1])]
     for i, ref in enumerate((su, sd, qu, qd)):
         copies.append(pltpu.make_async_copy(st.at[pl.ds(16 * i, 16)], ref, sem.at[2 + i]))
     for copy in copies:
         copy.start()
+    cn[...] = nout[0:8].astype(BF16)
+    sn[...] = nout[8:9, 0:16]
+    qn[...] = nout[16:17, 0:16]
     for copy in copies:
         copy.wait()
 
@@ -498,12 +504,13 @@
     hbm = pl.BlockSpec(memory_space=pl.ANY)
     sds = jax.ShapeDtypeStruct
     dma = pltpu.SemaphoreType.DMA
-    wide = lambda v: jnp.pad(v.reshape(1, 16), ((0, 0), (0, 1008)))
-    own = jnp.concatenate([mu, md.T, vu, vd.T, pn.astype(F32), wide(mn), wide(vn), jnp.zeros((5, 1024), F32)], axis=0)
+    parts = (mu, md.T, vu, vd.T, pn.astype(F32), mn.reshape(1, 16), vn.reshape(1, 16))
+    at = (0, 16, 32, 48, 64, 65, 66)
+    own = sum(jnp.pad(v, ((i, 72 - i - v.shape[0]), (0, 1024 - v.shape[1]))) for i, v in zip(at, parts))
     up, down, state = sds((NZ, NY, NC, 16, 1024), BF16), sds((1024, 1024), BF16), sds((16, 1024), F32)
     out_u, out_d, states, nout = pl.pallas_call(
         kernel,
-        out_shape=(up, down, sds((64, 1024), F32), sds((24, 1024), F32)),
+        out_shape=(up, down, sds((64, 1024), F32), sds((24, 128), F32)),
         in_specs=[vm, hbm, hbm],
         out_specs=(vm,) * 4,
         scratch_shapes=[
@@ -540,18 +547,17 @@
         ),
         name="update",
     )(own, pu.reshape(NZ, NY, NC, 16, 1024), pd.reshape(2, 512, 1024))
-    cu, cd, su, sd, qu, qd = pl.pallas_call(
+    cu, cd, su, sd, qu, qd, cn, sn, qn = pl.pallas_call(
         finish,
-        out_shape=(up, down, state, state, state, state),
-        in_specs=[vm] * 3,
-        out_specs=(hbm,) * 6,
+        out_shape=(up, down, state, state, state, state, sds((8, 128), BF16), sds((1, 16), F32), sds((1, 16), F32)),
+        in_specs=[vm] * 4,
+        out_specs=(hbm,) * 6 + (vm,) * 3,
         scratch_shapes=[dma((6,))],
         compiler_params=pltpu.CompilerParams(vmem_limit_bytes=2**20),
         name="finish",
-    )(out_u, out_d, states)
+    )(out_u, out_d, states, nout)
     return (
-        cu.reshape(1024, 1024), cd, nout[0].astype(BF16),
-        su, sd.T, nout[8, :16], qu, qd.T, nout[16, :16],
+        cu.reshape(1024, 1024), cd, cn.reshape(1024), su, sd.T, sn.reshape(16), qu, qd.T, qn.reshape(16),
     )
 
 

time: 82.6 us -> 73.6 us (0.89)
  local copies, waits for them, and re-layouts: 6.53 us -> 0 us
  Pallas kernels: 75.1 us -> 71.8 us
  other arithmetic: 0 us -> 0.99 us
    concatenate x1 -> x0, local copies, waits for them, and re-layouts: 4.09 us -> none  [local(): jnp.concatenate([mu, md.T, vu, vd.T, pn.astype(F32), wide(mn), wide(vn),...]
    pallas_call x1, Pallas kernels: 73 us -> 69.1 us  [local(): pl.pallas_call(kernel, out_shape=(up, down, sds((64, 1024), F32), sds((24...]
    pad x2 -> x0, local copies, waits for them, and re-layouts: 1.32 us -> none  [local(): wide = lambda v: jnp.pad(v.reshape(1, 16), ((0, 0), (0, 1008)))]
    add x0 -> x1, other arithmetic: none -> 0.99 us  [local(): sum((jnp.pad(v, ((i, 72 - i - v.shape[0]), (0, 1024 - v.shape[1]))) for i...]
where the time goes in v3:
time: 73.6 us; the launch traced here: 73.5 us
  Pallas kernels  71.8 us (98%)
  other arithmetic  0.99 us (1%)
    pallas_call x1, Pallas kernels, local(): pl.pallas_call(kernel, out_shape=(up, down, sds((64, 1024), F32), sds((24...  69.1 us
    pallas_call x1, Pallas kernels, local(): pl.pallas_call(finish, out_shape=(up, down, state, state, state, state, s...  2.71 us

profile of v3, /device:TPU:1, one launch (start us, length us, event | category | flops | bytes accessed | tf_op | source)
XLA Modules:
  0.0 73.5 jit_solution(10723125017106921760)
XLA Ops:
  0.6 1.0 %pad_add_fusion.own = f32[72,1024]{1,0:T(8,128)S(1)} fusion(f32[1,16]{1,0:T(1,128)} %bitcast.16, f32[1,16]{1,0:T(1,128)} %bitcast.17, f32[16,1024]{1,0:T(8,128)} %bitcast.14, f32[16,1024]{1,0:T(8,128)} %param.15, f32[16,1024]{1,0:T(8,128)} %bitcast.15, f32[16,1024]{1,0:T(8,128)} %param.12, bf16[1,1024]{1,0:T(2,128)(2,1)} %param.11), kind=kLoop, calls=%fused_computation | loop fusion | flops 516096 | bytes 559232 | tf_op jit(solution)/shard_map/add | solution.py:509
  1.6 69.1 %update.1 = (bf16[8,4,2,16,1024]{4,3,2,1,0:T(8,128)(2,1)S(1)}, bf16[1024,1024]{1,0:T(8,128)(2,1)S(1)}, f32[64,1024]{1,0:T(8,128)S(1)}, f32[24,128]{1,0:T(8,128)S(1)}) custom-call(f32[72,1024]{1,0:T(8,128)S(1)} %pad_add_fusion.own, bf16[8,4,2,16,1024]{4,3,2,1,0:T(8,128)(2,1)} %bitcast.12, bf16[2,512,1024]{2,1,0:T(8,128)(2,1)} %bitcast.13), custom_call_target="tpu_custom_call" | custom-call | tf_op jit(solution)/shard_map/update/pallas_call | solution.py:511
  70.8 2.7 %finish.1 = (bf16[8,4,2,16,1024]{4,3,2,1,0:T(8,128)(2,1)}, bf16[1024,1024]{1,0:T(8,128)(2,1)}, f32[16,1024]{1,0:T(8,128)}, f32[16,1024]{1,0:T(8,128)}, f32[16,10...) custom-call(bf16[8,4,2,16,1024]{4,3,2,1,0:T(8,128)(2,1)S(1)} %get-tuple-eleme, ...), custom_call_target="tpu_custom_call" | custom-call | tf_op jit(solution)/shard_map/finish/pallas_call | solution.py:550

commit v4 on v3

--- a/solution.py
+++ b/solution.py
@@ -139,56 +139,65 @@
             dp_0=zo(sign(direction)),
         )
 
-    def u_slot(direction, i):
-        k, h = yslots[i]
-        k = k * sign(direction)
-        kk = 2 if k == -2 else k
-        need_u(kk)
-        part = pl.ds(half_of(direction, h) * 4, 4)
-        val = pu[part, yo(kk), c].astype(F32) + pr_u[part, yo(kk)].astype(F32)
-        if i >= 2:
-            arrived(ur.at[direction, i - 2], u_recv.at[direction, i - 2])
-            val = val + ur[direction, i - 2]
-        us[direction, i] = val
-        started(
-            us.at[direction, i], ur.at[direction, i], u_send.at[direction], u_recv.at[direction, i],
-            dp_1=yo(sign(direction)),
-        )
-
-    def z_slot(direction, i):
-        k, h = zslots[i]
-        k = k * sign(direction)
-        rows = pl.ds(half_of(direction, h) * 8, 8)
-        val = sum_u[zo(k), rows]
-        if i >= 2:
-            arrived(zr.at[direction, i - 2], z_recv.at[direction, i - 2])
-            val = val + zr[direction, i - 2]
-        zs[direction, i] = val
-        started(
-            zs.at[direction, i], zr.at[direction, i], z_send.at[direction], z_recv.at[direction, i],
-            dp_0=zo(sign(direction)),
-        )
+    def u_slot(p, i):
+        for direction in (0, 1):
+            k, h = yslots[i]
+            k = k * sign(direction)
+            kk = 2 if k == -2 else k
+            need_u(kk)
+            part = pl.ds(half_of(direction, h) * 4, 4)
+            val = pu[part, yo(kk), c, p].astype(F32) + pr_u[part, yo(kk), p].astype(F32)
+            if i >= 2:
+                arrived(ur.at[p, direction, i - 2], u_recv.at[p, direction, i - 2])
+                val = val + ur[p, direction, i - 2]
+            us[p, direction, i] = val
+            started(
+                us.at[p, direction, i], ur.at[p, direction, i], u_send.at[direction], u_recv.at[p, direction, i],
+                dp_1=yo(sign(direction)),
+            )
+
+    def z_slot(p, i):
+        for direction in (0, 1):
+            k, h = zslots[i]
+            k = k * sign(direction)
+            val = sum_u[p, zo(k), :, lanes(half_of(direction, h))]
+            if i >= 2:
+                arrived(zr.at[p, direction, i - 2], z_recv.at[p, direction, i - 2])
+                val = val + zr[p, direction, i - 2]
+            zs[p, direction, i] = val
+            started(
+                zs.at[p, direction, i], zr.at[p, direction, i], z_send.at[direction], z_recv.at[p, direction, i],
+                dp_0=zo(sign(direction)),
+            )
+
+    lanes = lambda h: pl.ds(512 * h, 512)
 
     for i in (0, 1):
         for direction in (0, 1):
             d_slot(direction, i)
-        for direction in (0, 1):
-            u_slot(direction, i)
-
+        u_slot(0, i)
     pair_d(2, -2, 1, -1)
     started(sms.at[0], smr.at[0], sm_send.at[0], sm_recv.at[0], dp_2=o)
+    pair_u(0)
     pair_d(0)
-    pair_u(0)
-    for i in (2, 3):
+
+    def d_step(i):
         for direction in (0, 1):
             d_slot(direction, i)
-    for direction in (0, 1):
-        u_slot(direction, 2)
-
-    arrived(smr.at[0], sm_recv.at[0])
-    sms[1] = sms[0] + smr[0]
-    for dy in range(1, NY):
-        started(sms.at[1], smr.at[dy], sm_send.at[1], sm_recv.at[dy], dp_1=yo(dy))
+
+    def norm_pair():
+        arrived(smr.at[0], sm_recv.at[0])
+        sms[1] = sms[0] + smr[0]
+        for dy in range(1, NY):
+            started(sms.at[1], smr.at[dy], sm_send.at[1], sm_recv.at[dy], dp_1=yo(dy))
+
+    def norm_y():
+        total = sms[1]
+        for dy in range(1, NY):
+            arrived(smr.at[dy], sm_recv.at[dy])
+            total = total + smr[dy]
+        sms[2] = total
+        norm_on(0)
 
     def norm_on(k):
         for direction in (0, 1):
@@ -199,71 +208,57 @@
                 i = 4 + 4 * direction + k
                 started(src, smr.at[i], sm_send.at[2 + direction], sm_recv.at[i], dp_0=zo(sign(direction)))
 
-    for i in (4, 5, 6):
-        for direction in (0, 1):
-            d_slot(direction, i)
-
-    need_u(0)
-    for h in (0, 1):
-        part = pl.ds(4 * h, 4)
-        val = pu[part, y, c].astype(F32) + pr_u[part, y].astype(F32)
-        for direction in (0, 1):
-            i = 2 if half_of(direction, 0) == h else 1
-            arrived(ur.at[direction, i], u_recv.at[direction, i])
-            val = val + ur[direction, i]
-        sum_u[part] = val
-    for i in (0, 1):
-        for direction in (0, 1):
-            z_slot(direction, i)
-
-    total = sms[1]
-    for dy in range(1, NY):
-        arrived(smr.at[dy], sm_recv.at[dy])
-        total = total + smr[dy]
-    sms[2] = total
-    norm_on(0)
-
-    need_d(0)
-    for h in (0, 1):
-        rows = pl.ds(256 * h, 256)
-        val = pd[c, rows, col(z)].astype(F32) + pr_d[z, rows].astype(F32)
-        for direction in (0, 1):
-            i = 6 if half_of(direction, 0) == h else 5
-            arrived(dr.at[direction, i], d_recv.at[direction, i])
-            val = val + dr[direction, i]
-        for b in (0, 1):
-            gs[:, :, pl.ds(256 * h + 128 * b, 128)] = val[128 * b : 128 * b + 128].T.reshape(NY * NC, 16, 128)
-    for dy in (2, 1, 3, 0):
-        for dc in range(NC):
-            if dy or dc:
-                yt, ct = yo(dy), lax.rem(c + dc, NC)
-                started(
-                    gs.at[yt * NC + ct], gr.at[c, dy], g_send.at[0], g_recv.at[dy, dc], dp_1=yt, dp_2=ct
-                )
-    gr[c, 0] = gs[y * NC + c]
-
-    def z_step(*steps):
-        for i in steps:
+    def u_final(p):
+        need_u(0)
+        for h in (0, 1):
+            part = pl.ds(4 * h, 4)
+            val = pu[part, y, c, p].astype(F32) + pr_u[part, y, p].astype(F32)
             for direction in (0, 1):
-                z_slot(direction, i)
-
-    lane = lax.broadcasted_iota(jnp.int32, (16, 128), 1)
+                i = 2 if half_of(direction, 0) == h else 1
+                arrived(ur.at[p, direction, i], u_recv.at[p, direction, i])
+                val = val + ur[p, direction, i]
+            sum_u[p, part] = val
+        z_slot(p, 0)
+        z_slot(p, 1)
+
+    def d_final():
+        need_d(0)
+        for h in (0, 1):
+            rows = pl.ds(256 * h, 256)
+            val = pd[c, rows, col(z)].astype(F32) + pr_d[z, rows].astype(F32)
+            for direction in (0, 1):
+                i = 6 if half_of(direction, 0) == h else 5
+                arrived(dr.at[direction, i], d_recv.at[direction, i])
+                val = val + dr[direction, i]
+            for b in (0, 1):
+                gs[:, :, pl.ds(256 * h + 128 * b, 128)] = val[128 * b : 128 * b + 128].T.reshape(NY * NC, 16, 128)
+        for dy in (2, 1, 3, 0):
+            for dc in range(NC):
+                if dy or dc:
+                    yt, ct = yo(dy), lax.rem(c + dc, NC)
+                    started(
+                        gs.at[yt * NC + ct], gr.at[c, dy], g_send.at[0], g_recv.at[dy, dc], dp_1=yt, dp_2=ct
+                    )
+        gr[c, 0] = gs[y * NC + c]
+
 
     def tp_send(which, mean, master):
+        n = mean.shape[0]
+        lane = lax.broadcasted_iota(jnp.int32, (n, 128), 1)
         own = jnp.sum(master * master, axis=1, keepdims=True)
         slope = jnp.sum(mean * mean, axis=1, keepdims=True)
-        tps[which] = jnp.where(lane < 64, own, slope)
+        tps[which, 0:n] = jnp.where(lane < 64, own, slope)
         for k in range(1, NX):
             started(
-                tps.at[which], tpr.at[which, k - 1], t_send.at[which], t_recv.at[which, k - 1],
-                tp=lax.rem(x + k, NX),
+                tps.at[which, pl.ds(0, n)], tpr.at[which, k - 1, pl.ds(0, n)], t_send.at[which],
+                t_recv.at[which, k - 1], tp=lax.rem(x + k, NX),
             )
 
-    def tp_total(which):
-        val = tps[which]
+    def tp_total(which, n):
+        val = tps[which, 0:n]
         for k in range(1, NX):
-            arrived(tpr.at[which, k - 1], t_recv.at[which, k - 1])
-            val = val + tpr[which, k - 1]
+            arrived(tpr.at[which, k - 1, pl.ds(0, n)], t_recv.at[which, k - 1])
+            val = val + tpr[which, k - 1, 0:n]
         return jnp.sqrt(val[:, 0:1]) * lax.rsqrt(val[:, 64:65] + 1e-06)
 
     def down_sum():
@@ -274,21 +269,20 @@
                     arrived(gr.at[cs, dy], g_recv.at[dy, dc])
         for h in (0, 1):
             sd[:, pl.ds(512 * h, 512)] = (gr[h, 0] + gr[h, 1] + gr[h, 2] + gr[h, 3]) * 0.125
-        tp_send(1, sd[...], md[...])
-
-    def up_sum():
+        tp_send(2, sd[...], md[...])
+
+    def up_sum(p):
         for h in (0, 1):
-            rows = pl.ds(8 * h, 8)
-            val = sum_u[z, rows]
+            val = sum_u[p, z, :, lanes(h)]
             for direction in (0, 1):
                 i = 6 if half_of(direction, 0) == h else 5
-                arrived(zr.at[direction, i], z_recv.at[direction, i])
-                val = val + zr[direction, i]
-            su[rows] = val * 0.125
-        tp_send(0, su[...], mu[...])
+                arrived(zr.at[p, direction, i], z_recv.at[p, direction, i])
+                val = val + zr[p, direction, i]
+            su[p, :, lanes(h)] = val * 0.125
+        tp_send(p, su[p], mu[8 * p : 8 * p + 8])
 
     def down_update():
-        stepped, state = updated(md[...], vd[...], sd[...] * tp_total(1))
+        stepped, state = updated(md[...], vd[...], sd[...] * tp_total(2, 16))
         state_out[16:32] = stepped
         state_out[48:64] = state
         turned = stepped.astype(BF16)
@@ -301,11 +295,13 @@
                     started(gds.at[ct], gd.at[y, c], gd_send.at[0], gd_recv.at[dy, dc], dp_1=yt, dp_2=ct)
         gd[y, c] = gds[c]
 
-    def up_update():
-        stepped, state = updated(mu[...], vu[...], su[...] * tp_total(0))
-        state_out[0:16] = stepped
-        state_out[32:48] = state
-        out_u[z, y, c] = stepped.astype(BF16)
+    def up_update(p):
+        rows = pl.ds(8 * p, 8)
+        stepped, state = updated(mu[rows], vu[rows], su[p] * tp_total(p, 8))
+        state_out[8 * p : 8 * p + 8] = stepped
+        state_out[32 + 8 * p : 40 + 8 * p] = state
+        out_u[z, y, c, p] = stepped.astype(BF16)
+        first_u(p)
 
     def norm_update():
         total = sms[2]
@@ -320,48 +316,46 @@
             mine = jnp.broadcast_to(rolled[i, pl.ds(z, 1)], (8, 128))
             nout[8 + 8 * i : 16 + 8 * i] = pltpu.roll(mine, back, 1)
 
-    lanes = lambda h: pl.ds(512 * h, 512)
-
-    def to_partner_u(zt, yt):
-        piece = out_u.at[zt, yt, c]
+    def to_partner_u(p, zt, yt):
+        piece = out_u.at[zt, yt, c, p]
         started(piece, piece, pair_send.at[0], pair_recv.at[0], dp_2=o)
 
-    def to_y(kz):
-        for direction in (0, 1):
-            piece = out_u.at[zo(kz), y, c]
+    def to_y(p, kz):
+        for direction in (0, 1):
+            piece = out_u.at[zo(kz), y, c, p]
             started(
-                piece, piece, agy_send.at[direction], agy_recv.at[direction, 0, kz % NZ], dp_1=yo(sign(direction))
+                piece, piece, agy_send.at[direction], agy_recv.at[p, direction, 0, kz % NZ], dp_1=yo(sign(direction))
             )
-        to_partner_u(zo(kz), y)
-
-    def to_z(direction, k):
+        to_partner_u(p, zo(kz), y)
+
+    def to_z(p, direction, k):
         s = sign(direction)
-        piece = out_u.at[zo(-s * k), y, c]
-        started(piece, piece, agz_send.at[direction], agz_recv.at[direction, k], dp_0=zo(s))
+        piece = out_u.at[zo(-s * k), y, c, p]
+        started(piece, piece, agz_send.at[direction], agz_recv.at[p, direction, k], dp_0=zo(s))
         if k:
             piece = piece.at[:, lanes(half_of(direction, 0))]
-        started(piece, piece, agz_send.at[direction], agz_recv.at[direction, k + 1], dp_0=zo(2 * s))
-
-    def z_came(direction, k):
-        piece = out_u.at[zo(-sign(direction) * k), y, c]
+        started(piece, piece, agz_send.at[direction], agz_recv.at[p, direction, k + 1], dp_0=zo(2 * s))
+
+    def z_came(p, direction, k):
+        piece = out_u.at[zo(-sign(direction) * k), y, c, p]
         if k == 4:
             piece = piece.at[:, lanes(half_of(direction, 0))]
-        arrived(piece, agz_recv.at[direction, k - 1])
-
-    def y_came(kz):
+        arrived(piece, agz_recv.at[p, direction, k - 1])
+
+    def y_came(p, kz):
         for direction in (0, 1):
             s = sign(direction)
-            piece = out_u.at[zo(kz), yo(-s), c]
-            arrived(piece, agy_recv.at[direction, 0, kz % NZ])
+            piece = out_u.at[zo(kz), yo(-s), c, p]
+            arrived(piece, agy_recv.at[p, direction, 0, kz % NZ])
             half = piece.at[:, lanes(direction)]
-            started(half, half, agy_send.at[direction], agy_recv.at[direction, 1, kz % NZ], dp_1=yo(s))
-            to_partner_u(zo(kz), yo(-s))
-
-    def y_far(kz):
-        for direction in (0, 1):
-            half = out_u.at[zo(kz), yo(2), c].at[:, lanes(direction)]
-            arrived(half, agy_recv.at[direction, 1, kz % NZ])
-        to_partner_u(zo(kz), yo(2))
+            started(half, half, agy_send.at[direction], agy_recv.at[p, direction, 1, kz % NZ], dp_1=yo(s))
+            to_partner_u(p, zo(kz), yo(-s))
+
+    def y_far(p, kz):
+        for direction in (0, 1):
+            half = out_u.at[zo(kz), yo(2), c, p].at[:, lanes(direction)]
+            arrived(half, agy_recv.at[p, direction, 1, kz % NZ])
+        to_partner_u(p, zo(kz), yo(2))
 
     def d_block(kz, h):
         return out_d.at[pl.ds(pl.multiple_of(c * 512 + h * 256, 256), 256), col(zo(kz))]
@@ -401,61 +395,78 @@
                 to_dz(direction, k, hh)
             to_partner_d(-sign(direction) * k, hh)
 
-    def first_u():
-        for direction in (0, 1):
-            to_z(direction, 0)
-        to_y(0)
-
-    def u_came(k):
-        for direction in (0, 1):
-            z_came(direction, k)
+    def first_u(p):
+        for direction in (0, 1):
+            to_z(p, direction, 0)
+        to_y(p, 0)
+
+    def u_came(p, k):
+        for direction in (0, 1):
+            z_came(p, direction, k)
             if k == 2:
-                to_z(direction, k)
-        if k < 4:
-            for direction in (0, 1):
-                to_y(-sign(direction) * k)
-        else:
-            to_y(4)
-
-    z_step(2, 3)
-    norm_on(1)
-    down_sum()
-    z_step(4, 5, 6)
-    down_update()
-    up_sum()
-    norm_on(2)
-    turn()
-    up_update()
-    first_u()
-    turn_rest()
-    d_came(1, 0)
-    y_came(0)
-    u_came(1)
-    norm_on(3)
-    u_came(2)
-    d_came(1, 1)
-    y_far(0)
-    d_came(2, 0)
-    for kz in (-1, 1):
-        y_came(kz)
-    u_came(3)
-    for kz in (-2, 2):
-        y_came(kz)
-    d_came(2, 1)
-    u_came(4)
-    for kz in (-1, 1):
-        y_far(kz)
-    norm_on(4)
-    norm_update()
-    d_came(3, 0)
-    for kz in (-2, 2):
-        y_far(kz)
-    for kz in (-3, 3, 4):
-        y_came(kz)
-    d_came(3, 1)
-    d_came(4, 0)
-    for kz in (-3, 3, 4):
-        y_far(kz)
+                to_z(p, direction, k)
+        for kz in ((-k, k) if k < 4 else (4,)):
+            to_y(p, kz)
+
+    events = []
+
+    def at(time, step, *args):
+        events.append((time, len(events), step, args))
+
+    for i, t in zip(range(2, 7), (5.2, 8.0, 10.8, 13.6, 16.4)):
+        at(t, d_step, i)
+    at(5.4, u_slot, 0, 2)
+    at(5.5, u_slot, 1, 0)
+    at(5.5, u_slot, 1, 1)
+    at(5.6, norm_pair)
+    at(10.9, u_final, 0)
+    at(13.7, u_slot, 1, 2)
+    at(14.5, z_slot, 0, 2)
+    at(14.6, z_slot, 0, 3)
+    at(18.5, z_slot, 0, 4)
+    at(18.6, z_slot, 0, 5)
+    at(19.2, u_final, 1)
+    at(19.3, norm_y)
+    at(22.0, z_slot, 0, 6)
+    at(22.2, d_final)
+    at(23.0, z_slot, 1, 2)
+    at(23.1, z_slot, 1, 3)
+    at(24.0, norm_on, 1)
+    at(26.0, up_sum, 0)
+    at(26.3, z_slot, 1, 4)
+    at(26.4, z_slot, 1, 5)
+    at(27.3, down_sum)
+    at(29.0, up_update, 0)
+    at(29.4, z_slot, 1, 6)
+    at(30.0, norm_on, 2)
+    at(30.5, down_update)
+    at(32.2, up_sum, 1)
+    at(34.5, turn)
+    at(35.2, up_update, 1)
+    at(35.3, turn_rest)
+    at(36.5, norm_on, 3)
+    at(41.0, norm_on, 4)
+    at(41.1, norm_update)
+    for p, t in ((0, 29.0), (1, 35.2)):
+        at(t + 3.0, y_came, p, 0)
+        at(t + 3.2, u_came, p, 1)
+        at(t + 4.0, u_came, p, 2)
+        at(t + 6.0, y_far, p, 0)
+        at(t + 7.2, u_came, p, 3)
+        at(t + 8.0, u_came, p, 4)
+        for kz in (-1, 1):
+            at(t + 6.0, y_came, p, kz)
+            at(t + 9.0, y_far, p, kz)
+        for kz in (-2, 2):
+            at(t + 7.3, y_came, p, kz)
+            at(t + 10.2, y_far, p, kz)
+        for kz in (-3, 3, 4):
+            at(t + 11.0, y_came, p, kz)
+            at(t + 14.0, y_far, p, kz)
+    for k, h, t in ((1, 0, 38.4), (1, 1, 40.0), (2, 0, 42.2), (2, 1, 43.8), (3, 0, 46.0), (3, 1, 47.4), (4, 0, 49.0)):
+        at(t, d_came, k, h)
+    for _, _, step, args in sorted(events, key=lambda e: e[:2]):
+        step(*args)
 
     def pair_came():
         arrived(out_u.at[:, :, o], pair_recv.at[0])
@@ -474,13 +485,14 @@
     left(smr.at[pl.ds(0, 3)], sm_send.at[3])
     left(gs.at[pl.ds(0, 7)], g_send.at[0])
     left(pr_d.at[0, pl.ds(0, 448)], gd_send.at[0])
+    left(tpr.at[2], t_send.at[2])
     left(out_u.at[:, :, c], pair_send.at[0])
     left(out_d.at[pl.ds(pl.multiple_of(c * 512, 512), 512)], pair_send.at[1])
     for direction in (0, 1):
         left(ds.at[direction], d_send.at[direction])
-        left(us.at[direction], u_send.at[direction])
-        left(zs.at[direction], z_send.at[direction])
-        left(tpr.at[direction], t_send.at[direction])
+        left(us.at[:, direction], u_send.at[direction])
+        left(zs.at[:, direction], z_send.at[direction])
+        left(tpr.at[direction, :, pl.ds(0, 8)], t_send.at[direction])
         left(pr_d.at[0, pl.ds(0, 448)], agz_send.at[direction])
         left(pr_d.at[pl.ds(0, 3)], agy_send.at[direction])
         left(pr_d.at[pl.ds(0, 7), pl.ds(0, 256)], agd_send.at[direction])
@@ -507,46 +519,46 @@
     parts = (mu, md.T, vu, vd.T, pn.astype(F32), mn.reshape(1, 16), vn.reshape(1, 16))
     at = (0, 16, 32, 48, 64, 65, 66)
     own = sum(jnp.pad(v, ((i, 72 - i - v.shape[0]), (0, 1024 - v.shape[1]))) for i, v in zip(at, parts))
-    up, down, state = sds((NZ, NY, NC, 16, 1024), BF16), sds((1024, 1024), BF16), sds((16, 1024), F32)
+    up, down, state = sds((NZ, NY, NC, 2, 8, 1024), BF16), sds((1024, 1024), BF16), sds((16, 1024), F32)
     out_u, out_d, states, nout = pl.pallas_call(
         kernel,
         out_shape=(up, down, sds((64, 1024), F32), sds((24, 128), F32)),
         in_specs=[vm, hbm, hbm],
         out_specs=(vm,) * 4,
         scratch_shapes=[
-            pltpu.VMEM((NZ, NY, NC, 16, 1024), BF16),
+            pltpu.VMEM((NZ, NY, NC, 2, 8, 1024), BF16),
             pltpu.VMEM((2, 512, 1024), BF16),
-            pltpu.VMEM((NZ, NY, 16, 1024), BF16),
+            pltpu.VMEM((NZ, NY, 2, 8, 1024), BF16),
             pltpu.VMEM((NZ, 512, 128), BF16),
             pltpu.VMEM((2, 7, 256, 128), F32),
             pltpu.VMEM((2, 7, 256, 128), F32),
-            pltpu.VMEM((2, 3, 4, 16, 1024), F32),
-            pltpu.VMEM((2, 3, 4, 16, 1024), F32),
-            pltpu.VMEM((NZ, 16, 1024), F32),
-            pltpu.VMEM((2, 7, 8, 1024), F32),
-            pltpu.VMEM((2, 7, 8, 1024), F32),
+            pltpu.VMEM((2, 2, 3, 4, 8, 1024), F32),
+            pltpu.VMEM((2, 2, 3, 4, 8, 1024), F32),
+            pltpu.VMEM((2, NZ, 8, 1024), F32),
+            pltpu.VMEM((2, 2, 7, 8, 512), F32),
+            pltpu.VMEM((2, 2, 7, 8, 512), F32),
             pltpu.VMEM((8, 16, 512), F32),
             pltpu.VMEM((2, 4, 16, 512), F32),
-            pltpu.VMEM((2, 16, 128), F32),
-            pltpu.VMEM((2, 3, 16, 128), F32),
+            pltpu.VMEM((3, 16, 128), F32),
+            pltpu.VMEM((3, 3, 16, 128), F32),
             pltpu.VMEM((2, 16, 512), BF16),
             pltpu.VMEM((4, 2, 16, 512), BF16),
             pltpu.VMEM((3, 24, 128), F32),
             pltpu.VMEM((11, 24, 128), F32),
             pltpu.VMEM((2, 8, 128), F32),
-            pltpu.VMEM((16, 1024), F32),
+            pltpu.VMEM((2, 8, 1024), F32),
             pltpu.VMEM((16, 1024), F32),
             dma((2,)), dma((2,)), dma((4,)), dma((8,)),
-            dma((2,)), dma((2, 7)), dma((2,)), dma((2, 3)), dma((2,)), dma((2, 7)),
-            dma((1,)), dma((4, 2)), dma((2,)), dma((2, 3)), dma((4,)), dma((11,)),
-            dma((2,)), dma((2, 4)), dma((2,)), dma((2, 2, 8)), dma((2,)), dma((2, 4, 2)),
+            dma((2,)), dma((2, 7)), dma((2,)), dma((2, 2, 3)), dma((2,)), dma((2, 2, 7)),
+            dma((1,)), dma((4, 2)), dma((3,)), dma((3, 3)), dma((4,)), dma((11,)),
+            dma((2,)), dma((2, 2, 4)), dma((2,)), dma((2, 2, 2, 8)), dma((2,)), dma((2, 4, 2)),
             dma((1,)), dma((4, 2)), dma((2,)), dma((2,)),
         ],
         compiler_params=pltpu.CompilerParams(
             collective_id=0, has_side_effects=True, vmem_limit_bytes=VMEM_LIMIT
         ),
         name="update",
-    )(own, pu.reshape(NZ, NY, NC, 16, 1024), pd.reshape(2, 512, 1024))
+    )(own, pu.reshape(NZ, NY, NC, 2, 8, 1024), pd.reshape(2, 512, 1024))
     cu, cd, su, sd, qu, qd, cn, sn, qn = pl.pallas_call(
         finish,
         out_shape=(up, down, state, state, state, state, sds((8, 128), BF16), sds((1, 16), F32), sds((1, 16), F32)),

time: 73.6 us -> 74.4 us (1.011)
  Pallas kernels: 71.8 us -> 72.6 us
    pallas_call x1, Pallas kernels: 69.1 us -> 69.9 us  [local(): pl.pallas_call(kernel, out_shape=(up, down, sds((64, 1024), F32), sds((24...]
where the time goes in v4:
time: 74.4 us; the launch traced here: 74.3 us
  Pallas kernels  72.6 us (98%)
  other arithmetic  0.99 us (1%)
    pallas_call x1, Pallas kernels, local(): pl.pallas_call(kernel, out_shape=(up, down, sds((64, 1024), F32), sds((24...  69.9 us
    pallas_call x1, Pallas kernels, local(): pl.pallas_call(finish, out_shape=(up, down, state, state, state, state, s...  2.71 us

profile of v4, /device:TPU:1, one launch (start us, length us, event | category | flops | bytes accessed | tf_op | source)
XLA Modules:
  0.0 74.3 jit_solution(5947446823292662296)
XLA Ops:
  0.6 1.0 %pad_add_fusion.own = f32[72,1024]{1,0:T(8,128)S(1)} fusion(f32[1,16]{1,0:T(1,128)} %bitcast.16, f32[1,16]{1,0:T(1,128)} %bitcast.17, f32[16,1024]{1,0:T(8,128)} %bitcast.14, f32[16,1024]{1,0:T(8,128)} %param.15, f32[16,1024]{1,0:T(8,128)} %bitcast.15, f32[16,1024]{1,0:T(8,128)} %param.12, bf16[1,1024]{1,0:T(2,128)(2,1)} %param.11), kind=kLoop, calls=%fused_computation | loop fusion | flops 516096 | bytes 559232 | tf_op jit(solution)/shard_map/add | solution.py:521
  1.6 69.9 %update.1 = (bf16[8,4,2,2,8,1024]{5,4,3,2,1,0:T(8,128)(2,1)S(1)}, bf16[1024,1024]{1,0:T(8,128)(2,1)S(1)}, f32[64,1024]{1,0:T(8,128)S(1)}, f32[24,128]{1,0:T(8,128)S(1)}) custom-call(f32[72,1024]{1,0:T(8,128)S(1)} %pad_add_fusion.own, bf16[8,4,2,2,8,1024]{5,4,3,2,1,0:T(8,128)(2,1)} %bitcast.12, bf16[2,512,1024]{2,1,0:T(8,128)(2,1)} %bitcast.13), custom_call_target="tpu_custom_call" | custom-call | tf_op jit(solution)/shard_map/update/pallas_call | solution.py:523
  71.5 2.7 %finish.1 = (bf16[8,4,2,2,8,1024]{5,4,3,2,1,0:T(8,128)(2,1)}, bf16[1024,1024]{1,0:T(8,128)(2,1)}, f32[16,1024]{1,0:T(8,128)}, f32[16,1024]{1,0:T(8,128)}, f32[16...) custom-call(bf16[8,4,2,2,8,1024]{5,4,3,2,1,0:T(8,128)(2,1)S(1)} %get-tuple, ...), custom_call_target="tpu_custom_call" | custom-call | tf_op jit(solution)/shard_map/finish/pallas_call | solution.py:562
